TPU v7x, 32 devices: a whole 2x2x4 slice. The times are simulated.
32 devices in a mesh: section: 8 (over z, core), head: 4 (over y, x).
Axes of the slice: x: 2, y: 2, z: 4, core: 2. Of those that a mesh axis runs over, the one named last changes fastest.
Arguments:
- out_grad: bfloat16 [2048, 8192], P('section', 'head'), may hold values from -6 to 6
- held_query: bfloat16 [2048, 8192], P('section', 'head'), may hold values from -90 to 90
- held_output: bfloat16 [2048, 8192], P('section', 'head'), may hold values from -6 to 6
- key_cache: bfloat16 [10240, 512], P(('section', 'head')), may hold values from -4 to 4
- value_cache: bfloat16 [10240, 512], P(('section', 'head')), may hold values from -6 to 6
- segment_ids: int32 [2048], P('section'), may hold values from 0 to 127, never falling along the last dimension, each value on 1 to 64 neighbouring positions
- image_flags: int32 [2048], P('section'), may hold values 0 or 1
- cache_length: int32 [8], P('section'), may hold values from 1024 to 2048, as said below
- query_weight: bfloat16 [16384, 8192], P('section', 'head'), may hold values from -0.09375 to 0.09375
- kv_weight: bfloat16 [16384, 1024], P('section', 'head'), may hold values from -0.09375 to 0.09375
- norm_gain: bfloat16 [16384], P('section'), may hold values from 0.5 to 1.5
- layer_input: bfloat16 [2048, 4096], P(('section', 'head')), may hold values from -6 to 6
- residual_grad: bfloat16 [2048, 4096], P(('section', 'head')), may hold values from -3 to 3
Outputs:
- input_grad: bfloat16 [2048, 4096], P(('section', 'head'))
Inputs may be any that keep to these rules, and one draw needn't show every extreme that they name: `cache_length`: the two section indices 2 k and 2 k + 1 hold the same count; some section holds 2048.
All inputs are finite; a program needn't handle non-finite values. No bound on the sum of `image_flags` on one device may be relied on, other than what follows from the above.
Results may differ from a plain program's by a relative error of at most 0.0047.
Values may be sent and summed in bfloat16 or wider, within the bound.
No kernel may reach another device: no remote copies, remote signals or barrier semaphores. Data moves between devices by JAX's collectives and lax.ppermute only.
A program may use at most 128 MiB of HBM per device.

v0:
```python
import math

import jax
import jax.numpy as jnp
from jax import lax
from jax.sharding import PartitionSpec as P

KVH = 4
HD = 128
SL = 256
CTX = 2048


epsilon = 1e-06
far_negative = -1e30


def partner(value, axis, apart):
    return lax.ppermute(value, axis, [(i, i ^ 1 << apart) for i in range(lax.axis_size(axis))])


def contract_last(left, right):
    return lax.dot_general(
        left, right, (((1,), (1,)), ((), ())), preferred_element_type=jnp.float32
    )


def contract_first(left, right):
    return lax.dot_general(
        left, right, (((0,), (0,)), ((), ())), preferred_element_type=jnp.float32
    )


def heads_to_rows(array, local_heads):
    tokens = array.shape[0]
    return jnp.transpose(array.reshape(tokens, local_heads, HD), (1, 0, 2)).reshape(
        local_heads * tokens, HD
    )


def ordered(is_first, own_value, other_value, axis):
    return jnp.where(
        is_first,
        jnp.concatenate([own_value, other_value], axis),
        jnp.concatenate([other_value, own_value], axis),
    )


def body(
    out_grad,
    held_query,
    held_output,
    key_cache,
    value_cache,
    segment_ids,
    image_flags,
    cache_length,
    query_weight,
    kv_weight,
    norm_gain,
    layer_input,
    residual_grad,
):
    head_count = lax.axis_size("head")
    section_count = lax.axis_size("section")
    section_bits = section_count.bit_length() - 1
    parity = lax.axis_index("section") % 2
    is_first = parity == 0
    local_heads = out_grad.shape[1] // HD
    group_index = lax.axis_index("head") // (head_count // KVH)
    factor = 1.0 / math.sqrt(HD)
    stash_pair = jnp.stack([held_query, held_output])
    for bit_level in range(1, section_bits):
        stash_pair = partner(stash_pair, "section", bit_level)
    other_segments, other_flags = partner((segment_ids, image_flags), "section", 0)
    segments_all = ordered(is_first, segment_ids, other_segments, 0)
    flags_all = ordered(is_first, image_flags, other_flags, 0)
    pair_rows = jnp.stack([key_cache, value_cache])
    gathered = lax.all_gather(pair_rows, "head", axis=1, tiled=True)
    own_half = lax.dynamic_slice_in_dim(gathered, group_index * HD, HD, 2)
    other_half, other_gain = partner((own_half, norm_gain), "section", 0)
    both_halves = ordered(is_first, own_half, other_half, 1)
    key_rows = both_halves[0]
    value_rows = both_halves[1]
    gain_full = ordered(is_first, norm_gain, other_gain, 0)
    query_rows = heads_to_rows(stash_pair[0], local_heads)
    output_rows = heads_to_rows(stash_pair[1], local_heads)
    grad_rows = heads_to_rows(out_grad, local_heads)
    row_delta = jnp.sum(grad_rows.astype(jnp.float32) * output_rows.astype(jnp.float32), axis=1)
    token_here = parity * SL + jnp.tile(jnp.arange(SL, dtype=jnp.int32), local_heads)
    row_segments = jnp.tile(segment_ids, local_heads)
    row_flags = jnp.tile(image_flags, local_heads)
    key_block = math.gcd(CTX, 512)
    cache_blocks = CTX // key_block
    length = cache_length[0]

    def cache_scores(block_index):
        block_keys = lax.dynamic_slice_in_dim(key_rows, block_index * key_block, key_block, 0)
        block_values = lax.dynamic_slice_in_dim(value_rows, block_index * key_block, key_block, 0)
        scores = contract_last(query_rows, block_keys) * factor
        valid = block_index * key_block + jnp.arange(key_block, dtype=jnp.int32) < length
        return (jnp.where(valid[None, :], scores, far_negative), block_keys, block_values)

    slice_keys = key_rows[CTX:]
    slice_values = value_rows[CTX:]
    same_segment = row_segments[:, None] == segments_all[None, :]
    both_image = (row_flags[:, None] == 1) & (flags_all[None, :] == 1)
    slice_ok = same_segment & (
        (jnp.arange(2 * SL, dtype=jnp.int32)[None, :] <= token_here[:, None]) | both_image
    )
    slice_scores = jnp.where(slice_ok, contract_last(query_rows, slice_keys) * factor, far_negative)
    start_max = jnp.max(slice_scores, axis=1)
    start_sum = jnp.sum(jnp.exp(slice_scores - start_max[:, None]), axis=1)

    def first_pass(running, block_index):
        running_max, running_sum = running
        scores, unused_keys, unused_values = cache_scores(block_index)
        new_max = jnp.maximum(running_max, jnp.max(scores, axis=1))
        running_sum = running_sum * jnp.exp(running_max - new_max) + jnp.sum(
            jnp.exp(scores - new_max[:, None]), axis=1
        )
        return ((new_max, running_sum), None)

    (final_max, final_sum), unused_out = lax.scan(
        first_pass, (start_max, start_sum), jnp.arange(cache_blocks)
    )
    log_total = final_max + jnp.log(final_sum)

    def gradient_terms(scores, block_keys, block_values):
        attn_probs = jnp.exp(scores - log_total[:, None])
        prob_grad = contract_last(grad_rows, block_values)
        score_grad = (attn_probs * (prob_grad - row_delta[:, None]) * factor).astype(jnp.bfloat16)
        return (
            attn_probs,
            score_grad,
            jnp.dot(score_grad, block_keys, preferred_element_type=jnp.float32),
        )

    slice_probs, slice_grad, slice_term = gradient_terms(slice_scores, slice_keys, slice_values)

    def second_pass(running, block_index):
        scores, block_keys, block_values = cache_scores(block_index)
        unused_probs, unused_grad, block_term = gradient_terms(scores, block_keys, block_values)
        return (running + block_term, None)

    query_total, unused_out = lax.scan(second_pass, slice_term, jnp.arange(cache_blocks))
    query_grad = jnp.transpose(
        query_total.astype(jnp.bfloat16).reshape(local_heads, SL, HD), (1, 0, 2)
    ).reshape(SL, local_heads * HD)
    key_grad = contract_first(slice_grad, query_rows)
    value_grad = contract_first(slice_probs.astype(jnp.bfloat16), grad_rows)
    kv_width = 2 * KVH * HD
    column_width = kv_width // head_count
    sharers = head_count // KVH
    member = lax.axis_index("head") % sharers
    piece_width = HD // sharers
    current = jnp.stack([key_grad, value_grad], 1).reshape(2 * SL, 2, sharers, piece_width)
    level_count = sharers.bit_length() - 1
    for bit_level in reversed(range(level_count)):
        half = current.shape[2] // 2
        lower_part = current[:, :, :half]
        upper_part = current[:, :, half:]
        high_side = member // (1 << bit_level) % 2 == 1
        kept = jnp.where(high_side, upper_part, lower_part)
        sent = jnp.where(high_side, lower_part, upper_part)
        current = kept + partner(sent, "head", bit_level)
    kv_columns = current.reshape(2 * SL, 2 * piece_width)
    kv_total = kv_columns + partner(kv_columns, "section", 0)
    kv_part = kv_total.astype(jnp.bfloat16)
    collected_kv = lax.all_gather(kv_part, "head", axis=1, tiled=True)
    arranged = jnp.transpose(
        collected_kv.reshape(2 * SL, KVH, sharers, 2, piece_width), (0, 3, 1, 2, 4)
    ).reshape(2 * SL, kv_width)
    kv_rounded = lax.dynamic_slice_in_dim(
        arranged, lax.axis_index("head") * column_width, column_width, 1
    )
    other_query_w, other_kv_w = partner((query_weight, kv_weight), "section", 0)
    query_full = ordered(is_first, query_weight, other_query_w, 0)
    kv_full = ordered(is_first, kv_weight, other_kv_w, 0)
    own_kv = lax.dynamic_slice_in_dim(kv_rounded, parity * SL, SL, 0)
    normed_grad = lax.psum_scatter(
        contract_last(query_grad, query_full) + contract_last(own_kv, kv_full),
        "head",
        scatter_dimension=0,
        tiled=True,
    )
    values_in = layer_input.astype(jnp.float32)
    inverse = lax.rsqrt(jnp.mean(values_in * values_in, axis=1, keepdims=True) + epsilon)
    weighted = gain_full.astype(jnp.float32)[None, :] * normed_grad
    result = (
        residual_grad.astype(jnp.float32)
        + inverse * weighted
        - values_in * inverse**3 * jnp.mean(weighted * values_in, axis=1, keepdims=True)
    )
    return result.astype(jnp.bfloat16)


def solution(mesh):
    return jax.shard_map(
        body,
        mesh=mesh,
        in_specs=(
            P("section", "head"),
            P("section", "head"),
            P("section", "head"),
            P(("section", "head"), None),
            P(("section", "head"), None),
            P("section"),
            P("section"),
            P("section"),
            P("section", "head"),
            P("section", "head"),
            P("section"),
            P(("section", "head"), None),
            P(("section", "head"), None),
        ),
        out_specs=P(("section", "head"), None),
        check_vma=False,
    )
```

profile of v0, /device:TPU:0, one launch (start us, length us, event | category | flops | bytes accessed | tf_op | source)
XLA Modules:
  0.0 350.9 jit_solution(13112001818701966841)
XLA Ops:
  6.5 2.1 pad_maximum_fusion.1
  8.7 1.7 pad_maximum_fusion
  10.4 3.1 collective-permute-start.3
  13.6 45.7 %collective-permute-done.3 = bf16[2,256,2048]{2,1,0:T(8,128)(2,1)} collective-permute-done((bf16[2,256,2048]{2,1,0:T(8,128)(2,1)S(1)}, bf16[2,256,2048]{2,1,0:T(8,128)(2,1)}, u32[]{:S(2)}, u32[]{:S(2)}) %collective-permute-start.3) | collective-permute-done | bytes 2097184 | tf_op jit(solution)/shard_map/ppermute | solution.py:19
  59.3 2.8 collective-permute-start.4
  63.2 1.2 constant_dynamic-slice_fusion
  64.4 0.5 collective-permute-start.5
  65.0 87.3 %collective-permute-done.4 = bf16[2,256,2048]{2,1,0:T(8,128)(2,1)} collective-permute-done((bf16[2,256,2048]{2,1,0:T(8,128)(2,1)}, bf16[2,256,2048]{2,1,0:T(8,128)(2,1)}, u32[]{:S(2)}, u32[]{:S(2)}) %collective-permute-start.4) | collective-permute-done | bytes 2097184 | tf_op jit(solution)/shard_map/ppermute | solution.py:19
  152.2 1.8 convert_bitcast_fusion
  154.4 1.1 fusion.36
  156.4 1.3 slice_bitcast_fusion.1
  157.8 3.5 %fusion.53 = (f32[4096]{0:T(1024)S(1)}, f32[4096,512]{0,1:T(8,128)S(1)}) fusion(bf16[4096,128]{1,0:T(8,128)(2,1)S(1)} %bitcast.98, bf16[2,2560,128]{2,1,0:T(8,128)(2,1)S(1)} %maximum_select_fusion.6, pred[512]{0:T(512)(128)(4,1)S(1)} %fusion.50, pred[4096]{0:T(1024)(128)(4,1)S(1)} %eq.53, s32[4096]{0:T(1024)S(1)} %bitcast.116, s32[512]{0:T(512)S(1)} %add_select_fusion, ...), kind=kOutput, calls=%fused_computation.90 | convolution fusion | flops 553644032 | bytes 9624064 | tf_op jit(solution)/shard_map/dot_general | solution.py:23
  161.3 1.3 exponential_reduce_fusion.1
  162.7 1.9 copy-done.2
  164.6 25.4 %while.22 = (s32[]{:T(128)}, f32[4096]{0:T(1024)S(1)}, f32[4096]{0:T(1024)S(1)}, s32[4]{0:T(128)S(1)}, s32[]{:T(128)}, /*index=5*/bf16[2560,128]{1,0:T(8,128)(2,...) while((s32[]{:T(128)}, f32[4096]{0:T(1024)S(1)}, ...), condition=%wide.region_6.7_spmd, body=%wide.region_3.6_spmd.sunk | while | flops 551560192 | bytes 18171580 | solution.py:124
  164.6 0.6 dynamic_slice.46
  165.8 0.7 add_compare_fusion.4
  166.5 2.3 fusion.75
  168.8 2.1 exponential_reduce_fusion.3
  170.9 0.6 dynamic_slice.46
  172.2 0.7 add_compare_fusion.4
  172.8 2.3 fusion.75
  175.1 2.1 exponential_reduce_fusion.3
  177.3 0.6 dynamic_slice.46
  178.5 0.7 add_compare_fusion.4
  179.2 2.3 fusion.75
  181.5 2.1 exponential_reduce_fusion.3
  183.6 0.6 dynamic_slice.46
  184.9 0.7 add_compare_fusion.4
  185.5 2.3 fusion.75
  187.8 2.1 exponential_reduce_fusion.3
  190.0 4.7 %fusion.22 = bf16[4096,512]{0,1:T(8,128)(2,1)S(1)} fusion(f32[4096,512]{0,1:T(8,128)} %copy-done.2, bf16[4096,128]{1,0:T(8,128)(2,1)S(1)} %bitcast.100, f32[4096]{0:T(1024)S(1)} %bitcast.113, f32[4096]{0:T(1024)S(1)} %log_add_fusion, bf16[2,2560,128]{2,1,0:T(8,128)(2,1)S(1)} %maximum_select_fusion.6), kind=kOutput, calls=%fused_computation.29 | convolution fusion | flops 547356672 | bytes 13795328 | tf_op jit(solution)/shard_map/dot_general | solution.py:23
  194.7 1.5 convolution_bitcast_fusion
  196.2 1.5 fusion.38
  197.8 0.8 pad_maximum_fusion.2
  198.6 0.5 collective-permute-start.8
  199.1 3.5 fusion.47
  202.6 2.0 add_convert_fusion
  204.7 61.7 %while.23 = (s32[]{:T(128)}, f32[4096,128]{1,0:T(8,128)S(1)}, s32[4]{0:T(128)S(1)}, s32[]{:T(128)}, bf16[2560,128]{1,0:T(8,128)(2,1)}, /*index=5*/bf16[4096,128]...) while((s32[]{:T(128)}, f32[4096,128]{1,0:T(8,128)S(1)}, ...), condition=%wide.region_9.10_spmd, body=%wide.region_8.9_spmd.sunk | while | flops 1625818112 | bytes 23496916 | solution.py:146
  204.9 0.6 dynamic_slice.50
  206.2 0.7 add_compare_fusion.5
  206.8 5.4 %fusion.81 = f32[512,4096]{1,0:T(8,128)} fusion(bf16[4096,128]{1,0:T(8,128)(2,1)S(1)} %get-tuple-element.319, bf16[2560,128]{1,0:T(8,128)(2,1)} %get-tuple-element.318, s32[]{:T(128)S(6)} %select_n.162), kind=kOutput, calls=%fused_computation.12.clone.1 | convolution fusion | flops 536870912 | bytes 9568260 | tf_op jit(solution)/shard_map/while/body/eval_jaxpr/dot_general | solution.py:23
  212.2 8.2 %convolution_add_fusion.2 = f32[4096,128]{1,0:T(8,128)S(1)} fusion(f32[4096,128]{1,0:T(8,128)S(1)} %get-tuple-element.301, f32[512,4096]{1,0:T(8,128)} %fusion.81, bf16[4096,128]{1,0:T(8,128)(2,1)} %get-tuple-element.322, f32[4096]{0:T(1024)S(1)} %get-tuple-element.323, f32[4096]{0:T(1024)S(1)} %get-tuple-element.320, ...), kind=kOutput, calls=%fused_computation.9.clone.1 | convolution fusion | flops 1088946176 | bytes 13927936 | tf_op jit(solution)/shard_map/while/body/eval_jaxpr/dot_general | solution.py:136
  220.4 0.6 dynamic_slice.50
  221.7 0.7 add_compare_fusion.5
  222.3 5.4 %fusion.81 = f32[512,4096]{1,0:T(8,128)} fusion(bf16[4096,128]{1,0:T(8,128)(2,1)S(1)} %get-tuple-element.319, bf16[2560,128]{1,0:T(8,128)(2,1)} %get-tuple-element.318, s32[]{:T(128)S(6)} %select_n.162), kind=kOutput, calls=%fused_computation.12.clone.1 | convolution fusion | flops 536870912 | bytes 9568260 | tf_op jit(solution)/shard_map/while/body/eval_jaxpr/dot_general | solution.py:23
  227.7 8.0 %convolution_add_fusion.2 = f32[4096,128]{1,0:T(8,128)S(1)} fusion(f32[4096,128]{1,0:T(8,128)S(1)} %get-tuple-element.301, f32[512,4096]{1,0:T(8,128)} %fusion.81, bf16[4096,128]{1,0:T(8,128)(2,1)} %get-tuple-element.322, f32[4096]{0:T(1024)S(1)} %get-tuple-element.323, f32[4096]{0:T(1024)S(1)} %get-tuple-element.320, ...), kind=kOutput, calls=%fused_computation.9.clone.1 | convolution fusion | flops 1088946176 | bytes 13927936 | tf_op jit(solution)/shard_map/while/body/eval_jaxpr/dot_general | solution.py:136
  235.7 0.6 dynamic_slice.50
  237.0 0.7 add_compare_fusion.5
  237.6 5.4 %fusion.81 = f32[512,4096]{1,0:T(8,128)} fusion(bf16[4096,128]{1,0:T(8,128)(2,1)S(1)} %get-tuple-element.319, bf16[2560,128]{1,0:T(8,128)(2,1)} %get-tuple-element.318, s32[]{:T(128)S(6)} %select_n.162), kind=kOutput, calls=%fused_computation.12.clone.1 | convolution fusion | flops 536870912 | bytes 9568260 | tf_op jit(solution)/shard_map/while/body/eval_jaxpr/dot_general | solution.py:23
  243.0 8.0 %convolution_add_fusion.2 = f32[4096,128]{1,0:T(8,128)S(1)} fusion(f32[4096,128]{1,0:T(8,128)S(1)} %get-tuple-element.301, f32[512,4096]{1,0:T(8,128)} %fusion.81, bf16[4096,128]{1,0:T(8,128)(2,1)} %get-tuple-element.322, f32[4096]{0:T(1024)S(1)} %get-tuple-element.323, f32[4096]{0:T(1024)S(1)} %get-tuple-element.320, ...), kind=kOutput, calls=%fused_computation.9.clone.1 | convolution fusion | flops 1088946176 | bytes 13927936 | tf_op jit(solution)/shard_map/while/body/eval_jaxpr/dot_general | solution.py:136
  251.1 0.6 dynamic_slice.50
  252.3 0.7 add_compare_fusion.5
  253.0 5.4 %fusion.81 = f32[512,4096]{1,0:T(8,128)} fusion(bf16[4096,128]{1,0:T(8,128)(2,1)S(1)} %get-tuple-element.319, bf16[2560,128]{1,0:T(8,128)(2,1)} %get-tuple-element.318, s32[]{:T(128)S(6)} %select_n.162), kind=kOutput, calls=%fused_computation.12.clone.1 | convolution fusion | flops 536870912 | bytes 9568260 | tf_op jit(solution)/shard_map/while/body/eval_jaxpr/dot_general | solution.py:23
  258.4 8.0 %convolution_add_fusion.2 = f32[4096,128]{1,0:T(8,128)S(1)} fusion(f32[4096,128]{1,0:T(8,128)S(1)} %get-tuple-element.301, f32[512,4096]{1,0:T(8,128)} %fusion.81, bf16[4096,128]{1,0:T(8,128)(2,1)} %get-tuple-element.322, f32[4096]{0:T(1024)S(1)} %get-tuple-element.323, f32[4096]{0:T(1024)S(1)} %get-tuple-element.320, ...), kind=kOutput, calls=%fused_computation.9.clone.1 | convolution fusion | flops 1088946176 | bytes 13927936 | tf_op jit(solution)/shard_map/while/body/eval_jaxpr/dot_general | solution.py:136
  266.5 0.5 copy.23
  267.1 1.3 copy.24
  268.4 3.2 fusion.30
  271.6 15.1 %fusion.26 = f32[256,4096]{1,0:T(8,128)} fusion(f32[256,4096]{1,0:T(8,128)S(1)} %fusion.30, bf16[256,2048]{0,1:T(8,128)(2,1)S(1)} %bitcast.107, bf16[2048,2048]{1,0:T(8,128)(2,1)} %collective-permute-done.6, bf16[2048,2048]{1,0:T(8,128)(2,1)} %param.25, pred[]{:T(512)S(6)} %eq.46), kind=kOutput, calls=%fused_computation.37 | convolution fusion | flops 4371513344 | bytes 26214400 | tf_op jit(solution)/shard_map/dot_general | solution.py:23
  286.7 0.6 copy-done.9
  287.4 1.1 collective-permute-done
  288.5 52.0 %reduce-scatter.2.cloned.1.call-done = f32[64,4096]{1,0:T(8,128)} async-done(((f32[256,4096]{1,0:T(8,128)}), f32[64,4096]{1,0:T(8,128)}) %reduce-scatter.2.cloned.1.call-update) | async-done | bytes 1048592 | tf_op jit(solution)/shard_map/reduce_scatter | solution.py:181
  340.5 1.5 fusion.41
  342.0 2.4 fusion.44
  (74 shorter events, 2.8 us)
Async XLA Ops:
  6.5 56.1 %copy-start = (bf16[256,2048]{1,0:T(8,128)(2,1)S(1)}, bf16[256,2048]{1,0:T(8,128)(2,1)}, u32[]{:S(2)}) copy-start(bf16[256,2048]{1,0:T(8,128)(2,1)} %param.17) | copy-start | bytes 3145732
  6.5 55.5 %copy-start.10 = (s32[256]{0:T(256)S(1)}, s32[256]{0:T(256)}, u32[]{:S(2)}) copy-start(s32[256]{0:T(256)} %param.22) | copy-start | bytes 3076
  6.5 55.5 %copy-start.11 = (s32[256]{0:T(256)S(1)}, s32[256]{0:T(256)}, u32[]{:S(2)}) copy-start(s32[256]{0:T(256)} %param.23) | copy-start | bytes 3076
  6.5 56.7 %all-gather.3.cloned.1.call-start = ((), (), s32[]{:S(2)}) async-start(), calls=%async_computation.1 | async-start | bytes 3276800 | tf_op jit(solution)/shard_map/all_gather | solution.py:79
  8.7 258.4 %all-gather.5.cloned.1.call-start = ((), (), s32[]{:S(2)}) async-start(), calls=%async_computation.2 | async-start | bytes 1310720 | tf_op jit(solution)/shard_map/all_gather | solution.py:170
  10.4 48.9 %collective-permute-start.3 = (bf16[2,256,2048]{2,1,0:T(8,128)(2,1)S(1)}, bf16[2,256,2048]{2,1,0:T(8,128)(2,1)}, u32[]{:S(2)}, u32[]{:S(2)}) collective-permute-start(bf16[2,256,2048]{2,1,0:T(8,128)(2,1)S(1)} %pad_maximum_fusion), channel_id=1, source_target_pairs={{0,8},{4,12},{8,0},{12,4},{16,24},{20,28},{24,16},{28,20},{1,9},{5... | collective-permute-start | bytes 6291464 | tf_op jit(solution)/shard_map/ppermute | solution.py:19
  59.3 93.0 %collective-permute-start.4 = (bf16[2,256,2048]{2,1,0:T(8,128)(2,1)}, bf16[2,256,2048]{2,1,0:T(8,128)(2,1)}, u32[]{:S(2)}, u32[]{:S(2)}) collective-permute-start(bf16[2,256,2048]{2,1,0:T(8,128)(2,1)} %collective-permute-done.3), channel_id=1, source_target_pairs={{0,16},{4,20},{8,24},{12,28},{16,0},{20,4},{24,8},{28,12},{1,17},{... | collective-permute-start | bytes 6291464 | tf_op jit(solution)/shard_map/ppermute | solution.py:19
  62.1 1.2 collective-permute-start.1
  62.1 2.9 collective-permute-start.2
  62.6 209.0 %collective-permute-start.6 = (bf16[2048,2048]{1,0:T(8,128)(2,1)}, bf16[2048,2048]{1,0:T(8,128)(2,1)}, u32[]{:S(2)}, u32[]{:S(2)}) collective-permute-start(bf16[2048,2048]{1,0:T(8,128)(2,1)} %param.25), channel_id=1, source_target_pairs={{0,4},{4,0},{8,12},{12,8},{16,20},{20,16},{24,28},{28,24},{1,5},{5... | collective-permute-start | bytes 25165832 | tf_op jit(solution)/shard_map/ppermute | solution.py:19
  62.9 133.3 %copy-start.5 = (bf16[256,16,128]{2,0,1:T(8,128)(2,1)}, bf16[256,16,128]{2,0,1:T(8,128)(2,1)S(1)}, u32[]{:S(2)}) copy-start(bf16[256,16,128]{2,0,1:T(8,128)(2,1)S(1)} %copy_bitcast_fusion) | copy-start | bytes 3145732
  64.4 91.7 %collective-permute-start.5 = (bf16[2,1280,128]{2,1,0:T(8,128)(2,1)S(1)}, bf16[2,1280,128]{2,1,0:T(8,128)(2,1)S(1)}, u32[]{:S(2)}, u32[]{:S(2)}) collective-permute-start(bf16[2,1280,128]{2,1,0:T(8,128)(2,1)S(1)} %constant_dynamic-slice_fusion), channel_id=1, source_target_pairs={{0,4},{4,0},{8,12},{12,8},{16,20},{20,16},{24,28},{28,24},{1,5},{5... | collective-permute-start | bytes 1966088 | tf_op jit(solution)/shard_map/ppermute | solution.py:19
  156.4 33.5 %copy-start.6 = (bf16[2,2560,128]{2,1,0:T(8,128)(2,1)}, bf16[2,2560,128]{2,1,0:T(8,128)(2,1)S(1)}, u32[]{:S(2)}) copy-start(bf16[2,2560,128]{2,1,0:T(8,128)(2,1)S(1)} %maximum_select_fusion.6) | copy-start | bytes 3932164
  161.3 3.2 copy-start.2
  190.0 6.3 %copy-start.3 = (f32[4096,512]{0,1:T(8,128)S(1)}, f32[4096,512]{0,1:T(8,128)}, u32[]{:S(2)}) copy-start(f32[4096,512]{0,1:T(8,128)} %copy-done.2) | copy-start | bytes 25165828
  194.7 3.1 copy-start.4
  198.6 4.0 %collective-permute-start.7 = (f32[512,256]{0,1:T(8,128)}, f32[512,256]{0,1:T(8,128)}, u32[]{:S(2)}, u32[]{:S(2)}) collective-permute-start(f32[512,256]{0,1:T(8,128)} %bitcast.24), channel_id=1, source_target_pairs={{0,4},{4,0},{8,12},{12,8},{16,20},{20,16},{24,28},{28,24},{1,5},{5... | collective-permute-start | bytes 1572872 | tf_op jit(solution)/shard_map/ppermute | solution.py:19
  198.6 69.7 %collective-permute-start.8 = (bf16[2048,256]{1,0:T(8,128)(2,1)}, bf16[2048,256]{1,0:T(8,128)(2,1)}, u32[]{:S(2)}, u32[]{:S(2)}) collective-permute-start(bf16[2048,256]{1,0:T(8,128)(2,1)} %param.26), channel_id=1, source_target_pairs={{0,4},{4,0},{8,12},{12,8},{16,20},{20,16},{24,28},{28,24},{1,5},{5... | collective-permute-start | bytes 3145736 | tf_op jit(solution)/shard_map/ppermute | solution.py:19
  204.6 135.8 %reduce-scatter.2.cloned.1.call-start = ((), (), s32[]{:S(2)}) async-start(), calls=%async_computation.3 | async-start | bytes 5242880 | tf_op jit(solution)/shard_map/reduce_scatter | solution.py:181
  286.6 0.7 copy-start.9
  286.6 53.8 %copy-start.7 = (bf16[64,4096]{1,0:T(8,128)(2,1)S(1)}, bf16[64,4096]{1,0:T(8,128)(2,1)}, u32[]{:S(2)}) copy-start(bf16[64,4096]{1,0:T(8,128)(2,1)} %param.28) | copy-start | bytes 1572868
  286.6 55.4 %copy-start.8 = (bf16[64,4096]{1,0:T(8,128)(2,1)S(1)}, bf16[64,4096]{1,0:T(8,128)(2,1)}, u32[]{:S(2)}) copy-start(bf16[64,4096]{1,0:T(8,128)(2,1)} %param.29) | copy-start | bytes 1572868
  286.6 57.8 %copy-start.1 = (bf16[256,2048]{1,0:T(8,128)(2,1)S(1)}, bf16[256,2048]{1,0:T(8,128)(2,1)}, u32[]{:S(2)}) copy-start(bf16[256,2048]{1,0:T(8,128)(2,1)} %param.17) | copy-start | bytes 3145732
  287.3 1.2 collective-permute-start
Sparse Core Ops, SparseCore 0:
  9.2 42.2 all-gather.2
  204.8 27.4 all-gather.4
  286.8 53.6 reduce-scatter.1
where the time goes:
time: 352 us; the launch traced here: 351 us
  waiting for transfers between devices  186 us (53%)
  matrix products  95.8 us (27%)
  other arithmetic  28.9 us (8%)
  between operations  13.5 us (4%)
  local copies, waits for them, and re-layouts  13 us (4%)
  starting transfers between devices  7.6 us (2%)
  loops' own time  5.71 us (2%)
    ppermute x9, waiting for transfers between devices, partner(): lax.ppermute(value, axis, [(i, i ^ 1 << apart) for i in range(lax.axis_si...  134 us
    dot_general x12, matrix products, contract_last(): lax.dot_general(left, right, (((1,), (1,)), ((), ())), preferred_element_...  57.1 us
    reduce_scatter x1, waiting for transfers between devices, body(): lax.psum_scatter(contract_last(query_grad, query_full) + contract_last(ow...  52 us
    dot_general x5, matrix products, gradient_terms(): jnp.dot(score_grad, block_keys, preferred_element_type=jnp.float32)  35.6 us
    reduce_sum x4, other arithmetic, first_pass(): jnp.sum(jnp.exp(scores - new_max[:, None]), axis=1)  8.34 us
    ppermute x9, starting transfers between devices, partner(): lax.ppermute(value, axis, [(i, i ^ 1 << apart) for i in range(lax.axis_si...  7.52 us
  transfers between devices with their start and end apart: 12, of which 5 were waited for; matrix products, arithmetic and copies ran while one was open for 33% of the time, Pallas kernels for 0%

commit v1 on v0

v1 whole, which is shorter than its diff:
```python
import functools
import math

import jax
import jax.numpy as jnp
from jax import lax
from jax.experimental import pallas as pl
from jax.experimental.pallas import tpu as pltpu
from jax.sharding import PartitionSpec as P


KVH = 4
HD = 128
SL = 256
CTX = 2048

epsilon = 1e-06
far_negative = -1e30
factor = 1.0 / math.sqrt(HD)
log2_factor = factor * math.log2(math.e)

CHUNK_EIGHTHS = (4, 2, 2)
ROW_BLOCK = 512
KEY_BLOCK = 512
FEATURE_TILE = 512


NT = (((1,), (1,)), ((), ()))
TN = (((0,), (0,)), ((), ()))
NN = (((1,), (0,)), ((), ()))


def dot(left, right, dims):
    return lax.dot_general(left, right, dims, preferred_element_type=jnp.float32)


def xor_pairs(axis, mask):
    return [(i, i ^ mask) for i in range(lax.axis_size(axis))]


def inward_pairs(section_count):
    if section_count != 8:
        return []
    return [(0, 2), (1, 3), (6, 4), (7, 5)]


def chunk_plan(group_tokens):
    if group_tokens % 64:
        half = group_tokens // 2
        return [(0, half), (half, group_tokens - half)]
    plan, start = [], 0
    for eighths in CHUNK_EIGHTHS:
        count = group_tokens * eighths // 8
        plan.append((start, count))
        start += count
    return plan


def lane_tiles(values):
    return [values[:, j * HD:(j + 1) * HD] for j in range(values.shape[1] // HD)]


def fold(op, tiles):
    out = tiles[0]
    for tile in tiles[1:]:
        out = op(out, tile)
    return out


def attention_kernel(
    scal_ref, *refs, tokens, local_heads, head_count, paired,
):
    if paired:
        q_ref, o_ref, refs = refs[0].at[0], refs[0].at[1], refs[1:]
    else:
        q_ref, o_ref, refs = refs[0], refs[1], refs[2:]
    g_ref, cache_ref, slice_ref, bias_c_ref, bias_s_ref, prev_own_ref, prev_next_ref = refs[:7]
    own_ref, other_ref, kv_own_ref, kv_next_ref = refs[7:11]
    outs = refs[11:11 + head_count]
    s_ref, dq_ref, weights, groups, sems = refs[11 + head_count:]
    kc_ref, vc_ref = cache_ref.at[0], cache_ref.at[1]
    ks_ref, vs_ref = slice_ref.at[0], slice_ref.at[1]
    parity, head = scal_ref[0], scal_ref[1]
    heads = min(local_heads, max(1, ROW_BLOCK // tokens))
    blocks = local_heads // heads
    cache_blocks = CTX // KEY_BLOCK
    half, tile = weights.shape[1], groups.shape[2]
    tiles = half // tile
    count = tokens // head_count

    def weight_copy(side, index):
        rows = pl.ds(index * tile, tile)
        source = own_ref if side == 0 else other_ref
        return pltpu.make_async_copy(
            source.at[rows], weights.at[side, rows], sems.at[side * tiles + index]
        )

    for side in range(2):
        for index in range(tiles):
            weight_copy(side, index).start()
    kv_own_ref[...] = prev_own_ref[...]
    kv_next_ref[...] = prev_next_ref[...]

    def block(index, carry):
        def rows_of(ref):
            parts = [
                ref[..., pl.ds(pl.multiple_of((index * heads + j) * HD, HD), HD)].reshape(tokens, HD)
                for j in range(heads)
            ]
            return parts[0] if heads == 1 else jnp.concatenate(parts, axis=0)

        q_rows, g_rows = rows_of(q_ref), rows_of(g_ref)
        delta = jnp.sum(
            g_rows.astype(jnp.float32) * rows_of(o_ref).astype(jnp.float32), axis=1, keepdims=True
        )
        running = None
        for kb in range(cache_blocks):
            keys = slice(kb * KEY_BLOCK, (kb + 1) * KEY_BLOCK)
            scores = dot(q_rows, kc_ref[keys, :], NT)
            if (kb + 1) * KEY_BLOCK > CTX // 2:
                scores = scores + bias_c_ref[:, keys]
            s_ref[:, keys] = scores
            top = fold(jnp.maximum, lane_tiles(scores))
            running = top if running is None else jnp.maximum(running, top)
        bias = bias_s_ref[...].reshape(tokens, bias_s_ref.shape[-1])
        scores = dot(q_rows, ks_ref[...], NT) + (
            bias if heads == 1 else jnp.concatenate([bias] * heads, axis=0)
        )
        s_ref[:, CTX:] = scores
        running = jnp.maximum(running, fold(jnp.maximum, lane_tiles(scores)))
        shift = jnp.max(running, axis=1, keepdims=True) * log2_factor

        total = None
        query_grad = None
        for kb in range(cache_blocks):
            keys = slice(kb * KEY_BLOCK, (kb + 1) * KEY_BLOCK)
            probs = jnp.exp2(s_ref[:, keys] * log2_factor - shift)
            part = fold(jnp.add, lane_tiles(probs))
            total = part if total is None else total + part
            prob_grad = dot(g_rows, vc_ref[keys, :], NT)
            score_grad = (probs * (prob_grad - delta)).astype(jnp.bfloat16)
            term = dot(score_grad, kc_ref[keys, :], NN)
            query_grad = term if query_grad is None else query_grad + term
        probs = jnp.exp2(s_ref[:, CTX:] * log2_factor - shift)
        total = total + fold(jnp.add, lane_tiles(probs))
        scale = 1.0 / jnp.sum(total, axis=1, keepdims=True)
        probs = probs * scale
        prob_grad = dot(g_rows, vs_ref[...], NT)
        score_grad = (probs * (prob_grad - delta) * factor).astype(jnp.bfloat16)
        query_grad = query_grad * (scale * factor) + dot(score_grad, ks_ref[...], NN)
        key_grad = dot(q_rows, score_grad, TN)
        value_grad = dot(g_rows, probs.astype(jnp.bfloat16), TN)
        for ref, keys in ((kv_own_ref, slice(0, SL)), (kv_next_ref, slice(SL, 2 * SL))):
            ref[:HD, :] += key_grad[:, keys]
            ref[HD:, :] += value_grad[:, keys]
        query_grad = query_grad.astype(jnp.bfloat16)
        for j in range(heads):
            dq_ref[:, pl.ds(pl.multiple_of((index * heads + j) * HD, HD), HD)] = query_grad[
                j * tokens:(j + 1) * tokens
            ]
        return carry

    lax.fori_loop(0, blocks, block, 0)

    for side in range(2):

        def project(index, carry):
            weight_copy(side, index).wait()
            rows = pl.ds(pl.multiple_of(index * tile, tile), tile)
            result = dot(dq_ref[...], weights[side, rows, :], NT)
            for group in range(head_count):
                groups[group] = result[group * count:(group + 1) * count]
            place = parity if side == 0 else 1 - parity
            lanes = pl.ds(pl.multiple_of(place * half + index * tile, tile), tile)
            for d, out in enumerate(outs):
                out[:, lanes] = groups[head ^ d].astype(jnp.bfloat16)
            return carry

        lax.fori_loop(0, tiles, project, 0)


def whole_block(array):
    return pl.BlockSpec(array.shape, lambda step: (0,) * array.ndim)


def token_block(array, start, count, head_count):
    width = array.shape[1]
    grouped = array.reshape(head_count, array.shape[0] // head_count, width)
    if start % count == 0 and count % 16 == 0:
        return grouped, pl.BlockSpec((head_count, count, width), lambda step: (0, start // count, 0))
    rows = grouped[:, start:start + count].reshape(head_count * count, width)
    return rows, whole_block(rows)


def attention(scal, stash, grads, cache, current, bias_c, biases, prev, own, other, head_count):
    tokens, width = stash[0].shape[-2:]
    local_heads = width // HD
    heads = min(local_heads, max(1, ROW_BLOCK // tokens))
    keys = cache.shape[1] + current.shape[1]
    half = own.shape[0]
    tile = min(half, FEATURE_TILE)
    count = tokens // head_count
    operands = [(array, whole_block(array)) for array in stash]
    operands += [grads] + [(array, whole_block(array)) for array in (cache, current, bias_c)]
    operands += [biases] + [(array, whole_block(array)) for array in prev]
    operands += [(array, pl.BlockSpec(memory_space=pl.ANY)) for array in (own, other)]
    results = [jax.ShapeDtypeStruct(array.shape, jnp.float32) for array in prev]
    results += [jax.ShapeDtypeStruct((count, 2 * half), jnp.bfloat16) for _ in range(head_count)]
    outs = pl.pallas_call(
        functools.partial(
            attention_kernel,
            tokens=tokens,
            local_heads=local_heads,
            head_count=head_count,
            paired=len(stash) == 1,
        ),
        out_shape=results,
        grid=(1,),
        in_specs=[pl.BlockSpec(memory_space=pltpu.SMEM)] + [spec for _, spec in operands],
        out_specs=[whole_block(result) for result in results],
        scratch_shapes=[
            pltpu.VMEM((heads * tokens, keys), jnp.float32),
            pltpu.VMEM((tokens, width), jnp.bfloat16),
            pltpu.VMEM((2, half, width), jnp.bfloat16),
            pltpu.VMEM((head_count, count, tile), jnp.float32),
            pltpu.SemaphoreType.DMA((2 * (half // tile),)),
        ],
        compiler_params=pltpu.CompilerParams(vmem_limit_bytes=48 * 2**20),
        cost_estimate=pl.CostEstimate(
            flops=24 * tokens * local_heads * keys * HD,
            bytes_accessed=4 * tokens * width * 2 + keys * HD * 4 + 4 * half * width,
            transcendentals=tokens * local_heads * keys,
        ),
        name="attention",
    )(scal, *[array for array, _ in operands])
    return outs[:2], outs[2:]


def pack_kernel(q_ref, o_ref, *outs, plan, group_tokens, head_count):
    for out, (start, count) in zip(outs, plan):
        for group in range(head_count):
            rows = slice(group * group_tokens + start, group * group_tokens + start + count)
            out[0, group * count:(group + 1) * count] = q_ref[rows]
            out[1, group * count:(group + 1) * count] = o_ref[rows]


def pack(q, o, plan, group_tokens, head_count):
    tokens, width = q.shape
    lanes = min(width, 512)
    return pl.pallas_call(
        functools.partial(
            pack_kernel, plan=plan, group_tokens=group_tokens, head_count=head_count
        ),
        out_shape=[
            jax.ShapeDtypeStruct((2, head_count * count, width), q.dtype) for _, count in plan
        ],
        grid=(width // lanes,),
        in_specs=[pl.BlockSpec((tokens, lanes), lambda step: (0, step))] * 2,
        out_specs=[
            pl.BlockSpec((2, head_count * count, lanes), lambda step: (0, 0, step))
            for _, count in plan
        ],
        name="pack",
    )(q, o)


def share_kernel(scal_ref, own_ref, recv_ref, *outs):
    head = scal_ref[1]
    count = outs[0].shape[0]
    total = (own_ref[...] + recv_ref[...]).T
    head_count = len(outs)
    for d, out in enumerate(outs):
        for group in range(head_count):

            @pl.when((head ^ d) == group)
            def _():
                out[...] = total[group * count:(group + 1) * count].astype(out.dtype)


def share_kv(scal, own, recv, head_count, dtype):
    width, tokens = own.shape
    count = tokens // head_count
    results = [jax.ShapeDtypeStruct((count, width), dtype) for _ in range(head_count)]
    return pl.pallas_call(
        share_kernel,
        out_shape=results,
        grid=(1,),
        in_specs=[pl.BlockSpec(memory_space=pltpu.SMEM), whole_block(own), whole_block(recv)],
        out_specs=[whole_block(result) for result in results],
        cost_estimate=pl.CostEstimate(
            flops=tokens * width, bytes_accessed=tokens * width * 10, transcendentals=0
        ),
        name="share",
    )(scal, own, recv)


def finish_kernel(
    scal_ref, gain_ref, x_ref, res_ref, *refs, plan, head_count, shares, spent, columns
):
    kv_pieces, refs = refs[:head_count], refs[head_count:]
    pieces, refs = refs[:shares], refs[shares + spent:]
    sources, refs = refs[:2 * columns], refs[2 * columns:]
    out_ref, gathered, total_ref, weights, sems = refs
    parity, head = scal_ref[0], scal_ref[1]
    sharers = head_count // KVH
    half, width = sources[0].shape

    def weight_copy(index):
        return pltpu.make_async_copy(sources[index], weights.at[index], sems.at[index])

    for index in range(2 * columns):
        weight_copy(index).start()
    if sharers > 1:
        gathered[...] = jnp.zeros_like(gathered)
    for d, piece in enumerate(kv_pieces):
        group = (head ^ d) // sharers
        for part in range(2):
            lanes = pl.ds(pl.multiple_of(group * HD + part * KVH * HD, HD), HD)
            value = piece[:, part * HD:(part + 1) * HD].astype(jnp.float32)
            if sharers > 1:
                value = gathered[:, lanes] + value
            gathered[:, lanes] = value
    for c, (start, count) in enumerate(plan):
        rows = slice(start, start + count)
        total_ref[rows, :] = fold(
            jnp.add,
            [pieces[c * head_count + d][...].astype(jnp.float32) for d in range(head_count)],
        )
    x = x_ref[...].astype(jnp.float32)
    inverse = lax.rsqrt(jnp.mean(x * x, axis=1, keepdims=True) + epsilon)
    for index in range(2 * columns):
        side, column = index // columns, index % columns
        if columns == 1:
            left = gathered[...]
        else:
            left = gathered[:, pl.ds(pl.multiple_of((head ^ column) * width, width), width)]
        left = left.astype(jnp.bfloat16)
        place = parity if side == 0 else 1 - parity
        lanes = pl.ds(pl.multiple_of(place * half, half), half)
        weight_copy(index).wait()
        total_ref[:, lanes] += dot(left, weights[index], NT)
    weighted = gain_ref[...].astype(jnp.float32) * total_ref[...]
    mean = jnp.mean(weighted * x, axis=1, keepdims=True)
    out_ref[...] = (
        res_ref[...].astype(jnp.float32)
        + inverse * weighted
        - x * (inverse * inverse * inverse * mean)
    ).astype(out_ref.dtype)


def finish(scal, gain, x, residual, kv_pieces, pieces, spent, weights, plan):
    head_count = len(kv_pieces)
    half, width = weights[0].shape
    columns = len(weights) // 2
    rows = x.shape[0]
    local = [gain, x, residual, *kv_pieces, *pieces]
    remote = [*spent, *weights]
    return pl.pallas_call(
        functools.partial(
            finish_kernel,
            plan=plan,
            head_count=head_count,
            shares=len(pieces),
            spent=len(spent),
            columns=columns,
        ),
        out_shape=jax.ShapeDtypeStruct(x.shape, jnp.bfloat16),
        grid=(1,),
        in_specs=[pl.BlockSpec(memory_space=pltpu.SMEM)]
        + [whole_block(array) for array in local]
        + [pl.BlockSpec(memory_space=pl.ANY) for _ in remote],
        out_specs=whole_block(x),
        scratch_shapes=[
            pltpu.VMEM((rows, 2 * KVH * HD), jnp.float32),
            pltpu.VMEM((rows, 2 * half), jnp.float32),
            pltpu.VMEM((2 * columns, half, width), jnp.bfloat16),
            pltpu.SemaphoreType.DMA((2 * columns,)),
        ],
        compiler_params=pltpu.CompilerParams(vmem_limit_bytes=40 * 2**20),
        cost_estimate=pl.CostEstimate(
            flops=512 * half * width * columns,
            bytes_accessed=4 * half * width * columns,
            transcendentals=0,
        ),
        name="finish",
    )(scal, *local, *remote)


def body(
    out_grad,
    held_query,
    held_output,
    key_cache,
    value_cache,
    segment_ids,
    image_flags,
    cache_length,
    query_weight,
    kv_weight,
    norm_gain,
    layer_input,
    residual_grad,
):
    head_count = lax.axis_size("head")
    section_count = lax.axis_size("section")
    head = lax.axis_index("head")
    parity = lax.axis_index("section") % 2
    is_first = parity == 0
    sharers = head_count // KVH
    group_tokens = SL // head_count
    plan = chunk_plan(group_tokens)
    scal = jnp.stack([parity, head]).astype(jnp.int32)

    def rows_of_chunk(array, start, count):
        grouped = array.reshape(head_count, group_tokens, array.shape[1])
        return grouped[:, start:start + count].reshape(head_count * count, array.shape[1])

    def swap_cores(value):
        return lax.ppermute(value, "section", xor_pairs("section", 1))

    def ordered(own_value, other_value, axis):
        return jnp.where(
            is_first,
            jnp.concatenate([own_value, other_value], axis),
            jnp.concatenate([other_value, own_value], axis),
        )

    mirror = xor_pairs("section", section_count - 2)
    inward = inward_pairs(section_count)
    first = [rows_of_chunk(held_query, *plan[0]), rows_of_chunk(held_output, *plan[0])]
    first, (held_query, held_output) = lax.optimization_barrier((first, (held_query, held_output)))
    buffers = pack(held_query, held_output, plan[1:], group_tokens, head_count)
    buffers, (key_cache, value_cache, kv_weight, query_weight) = lax.optimization_barrier(
        (buffers, (key_cache, value_cache, kv_weight, query_weight))
    )
    stash, spent = [], []
    for c, group in enumerate([first] + [[buffer] for buffer in buffers]):
        stash.append([])
        for buffer in group:
            stash[-1].append(lax.ppermute(buffer, "section", mirror))
        for buffer in group:
            if inward and c + 1 < len(plan):
                spent.append(lax.ppermute(buffer, "section", inward))

    pair_rows = jnp.stack([key_cache, value_cache])
    rows_here = pair_rows.shape[1]
    own_half = jnp.zeros((2, head_count * rows_here, HD), jnp.bfloat16)
    for d in range(head_count):
        target = head ^ d
        piece = lax.dynamic_slice_in_dim(pair_rows, target // sharers * HD, HD, 2)
        if d:
            piece = lax.ppermute(piece, "head", xor_pairs("head", d))
        own_half = lax.dynamic_update_slice_in_dim(own_half, piece, target * rows_here, 1)
    other_half, other_gain = swap_cores((own_half, norm_gain))
    both = ordered(own_half, other_half, 1)
    gain = ordered(norm_gain, other_gain, 0)[None, :]
    cache_rows = both[:, :CTX]
    own_rows = lax.dynamic_slice_in_dim(both, CTX + parity * SL, SL, 1)
    next_rows = lax.dynamic_slice_in_dim(both, CTX + (1 - parity) * SL, SL, 1)
    slice_rows = jnp.concatenate([own_rows, next_rows], 1)

    other_segments, other_flags = swap_cores((segment_ids, image_flags))
    positions = jnp.arange(SL, dtype=jnp.int32)
    own_position = parity * SL + positions
    key_position = jnp.concatenate([own_position, (1 - parity) * SL + positions])
    key_segments = jnp.concatenate([segment_ids, other_segments])
    key_flags = jnp.concatenate([image_flags, other_flags])
    visible = (segment_ids[:, None] == key_segments[None, :]) & (
        (key_position[None, :] <= own_position[:, None])
        | ((image_flags[:, None] == 1) & (key_flags[None, :] == 1))
    )
    bias_s = jnp.where(visible, 0.0, far_negative).astype(jnp.float32)
    bias_c = jnp.where(
        jnp.arange(CTX, dtype=jnp.int32)[None, :] < cache_length[0], 0.0, far_negative
    ).astype(jnp.float32)

    other_weight = swap_cores(query_weight)
    column_width = kv_weight.shape[1]
    kv_columns = [kv_weight]
    for d in range(1, head_count):
        kv_columns.append(lax.ppermute(kv_weight, "head", xor_pairs("head", d)))
    if column_width % HD:
        kv_rows = jnp.zeros((kv_weight.shape[0], head_count * column_width), jnp.bfloat16)
        for d, piece in enumerate(kv_columns):
            kv_rows = lax.dynamic_update_slice_in_dim(kv_rows, piece, (head ^ d) * column_width, 1)
        kv_columns = [kv_rows]
    for d in range(len(kv_columns)):
        kv_columns.append(swap_cores(kv_columns[d]))

    kv_grad = [jnp.zeros((2 * HD, SL), jnp.float32)] * 2
    pieces = []
    for c, (start, count) in enumerate(plan):
        kv_grad, parts = attention(
            scal,
            stash[c],
            token_block(out_grad, start, count, head_count),
            cache_rows,
            slice_rows,
            bias_c,
            token_block(bias_s, start, count, head_count),
            kv_grad,
            query_weight,
            other_weight,
            head_count,
        )
        for d, part in enumerate(parts):
            pieces.append(lax.ppermute(part, "head", xor_pairs("head", d)) if d else part)
    received = swap_cores(kv_grad[1])
    share_dtype = jnp.bfloat16 if sharers == 1 else jnp.float32
    shares = list(share_kv(scal, kv_grad[0], received, head_count, share_dtype))
    for d in range(1, head_count):
        shares[d] = lax.ppermute(shares[d], "head", xor_pairs("head", d))
    return finish(
        scal, gain, layer_input, residual_grad, shares, pieces, spent, kv_columns, plan
    )


def solution(mesh):
    return jax.shard_map(
        body,
        mesh=mesh,
        in_specs=(
            P("section", "head"),
            P("section", "head"),
            P("section", "head"),
            P(("section", "head"), None),
            P(("section", "head"), None),
            P("section"),
            P("section"),
            P("section"),
            P("section", "head"),
            P("section", "head"),
            P("section"),
            P(("section", "head"), None),
            P(("section", "head"), None),
        ),
        out_specs=P(("section", "head"), None),
        check_vma=False,
    )
```

time: 352 us -> 212 us (0.60)
  waiting for transfers between devices: 186 us -> 43.3 us
  matrix products: 95.8 us -> 0 us
  starting transfers between devices: 7.6 us -> 72 us
  Pallas kernels: 0 us -> 60.8 us
  other arithmetic: 28.9 us -> 0.96 us
  local copies, waits for them, and re-layouts: 13 us -> 32.4 us
  between operations: 13.5 us -> 1.3 us
  loops' own time: 5.71 us -> 0 us
    dot_general x19 -> x0, matrix products: 95.8 us -> none  [the longest x12 57.1 us: contract_last(): lax.dot_general(left, right, (((1,), (1,)), ((), ())), preferred_element_...]
    ppermute x9 -> x35, waiting for transfers between devices: 134 us -> 43.3 us  [the longest x4 22.9 us: body(): stash[-1].append(lax.ppermute(buffer, 'section', mirror))]
    ppermute x9 -> x35, starting transfers between devices: 7.52 us -> 72 us  [the longest x3 38.1 us: body(): spent.append(lax.ppermute(buffer, 'section', inward))]
    pallas_call x0 -> x6, Pallas kernels: none -> 60.8 us  [the longest x3 48.9 us: attention(): pl.pallas_call(functools.partial(attention_kernel, tokens=tokens, local_h...]
    reduce_scatter x1 -> x0, waiting for transfers between devices: 52 us -> none  [body(): lax.psum_scatter(contract_last(query_grad, query_full) + contract_last(ow...]
    unnamed x30 -> x88, local copies, waits for them, and re-layouts: 3.23 us -> 29.2 us
    reduce_sum x7 -> x0, other arithmetic: 12.3 us -> none  [the longest x4 8.34 us: first_pass(): jnp.sum(jnp.exp(scores - new_max[:, None]), axis=1)]
    dynamic_slice x9 -> x1, local copies, waits for them, and re-layouts: 6.08 us -> 0.03 us  [body(): own_rows = lax.dynamic_slice_in_dim(both, CTX + parity * SL, SL, 1)]
  transfers between devices with their start and end apart: 12 -> 35, of which waited for: 5 -> 11; matrix products, arithmetic and copies ran while one was open for 33% -> 1% of each run, Pallas kernels for 0% -> 24%
where the time goes in v1:
time: 212 us; the launch traced here: 211 us
  starting transfers between devices  72 us (34%)
  Pallas kernels  60.8 us (29%)
  waiting for transfers between devices  43.3 us (20%)
  local copies, waits for them, and re-layouts  32.4 us (15%)
    pallas_call x3, Pallas kernels, attention(): pl.pallas_call(functools.partial(attention_kernel, tokens=tokens, local_h...  48.9 us
    ppermute x3, starting transfers between devices, body(): spent.append(lax.ppermute(buffer, 'section', inward))  38.1 us
    unnamed x88, local copies, waits for them, and re-layouts  29.2 us
    ppermute x4, waiting for transfers between devices, body(): stash[-1].append(lax.ppermute(buffer, 'section', mirror))  22.9 us
    ppermute x9, waiting for transfers between devices, body(): lax.ppermute(part, 'head', xor_pairs('head', d))  11.9 us
    ppermute x9, starting transfers between devices, body(): lax.ppermute(part, 'head', xor_pairs('head', d))  11.2 us
    ppermute x4, starting transfers between devices, body(): stash[-1].append(lax.ppermute(buffer, 'section', mirror))  10 us
    ppermute x3, waiting for transfers between devices, body(): piece = lax.ppermute(piece, 'head', xor_pairs('head', d))  7.48 us
  transfers between devices with their start and end apart: 35, of which 11 were waited for; matrix products, arithmetic and copies ran while one was open for 1% of the time, Pallas kernels for 24%

profile of v1, /device:TPU:0, one launch (start us, length us, event | category | flops | bytes accessed | tf_op | source)
XLA Modules:
  0.0 210.8 jit_solution(6389045812076577029)
XLA Ops:
  0.0 2.0 slice.12
  2.0 0.8 slice.13
  2.8 3.7 %pack.1 = (bf16[2,64,2048]{2,1,0:T(8,128)(2,1)}, bf16[2,64,2048]{2,1,0:T(8,128)(2,1)}) custom-call(bf16[256,2048]{1,0:T(8,128)(2,1)} %q_ref, bf16[256,2048]{1,0:T(8,128)(2,1)} %o_ref), custom_call_target="tpu_custom_call" | custom-call | tf_op jit(solution)/shard_map/pack/pallas_call | solution.py:250
  7.3 2.6 %collective-permute-start.2 = (bf16[2,320,128]{2,1,0:T(8,128)(2,1)S(1)}, bf16[2,320,128]{2,1,0:T(8,128)(2,1)S(1)}, u32[]{:S(2)}, u32[]{:S(2)}) collective-permute-start(bf16[2,320,128]{2,1,0:T(8,128)(2,1)S(1)} %get-tuple-element.77), channel_id=1, source_target_pairs={{0,1},{1,0},{2,3},{3,2},{4,5},{5,4},{6,7},{7,6},{8,9},{9,8},{10,11... | collective-permute-start | bytes 491528 | tf_op jit(solution)/shard_map/ppermute | solution.py:452
  9.9 1.5 collective-permute-start.3
  12.2 2.8 %collective-permute-done.2 = bf16[2,320,128]{2,1,0:T(8,128)(2,1)S(1)} collective-permute-done((bf16[2,320,128]{2,1,0:T(8,128)(2,1)S(1)}, bf16[2,320,128]{2,1,0:T(8,128)(2,1)S(1)}, u32[]{:S(2)}, u32[]{:S(2)}) %collective-permute-start.2) | collective-permute-done | bytes 163872 | tf_op jit(solution)/shard_map/ppermute | solution.py:452
  15.0 4.7 %collective-permute-done.3 = bf16[2,320,128]{2,1,0:T(8,128)(2,1)S(1)} collective-permute-done((bf16[2,320,128]{2,1,0:T(8,128)(2,1)S(1)}, bf16[2,320,128]{2,1,0:T(8,128)(2,1)S(1)}, u32[]{:S(2)}, u32[]{:S(2)}) %collective-permute-start.3) | collective-permute-done | bytes 163872 | tf_op jit(solution)/shard_map/ppermute | solution.py:452
  19.7 3.6 %collective-permute-start.10 = (bf16[128,2048]{1,0:T(8,128)(2,1)}, bf16[128,2048]{1,0:T(8,128)(2,1)S(1)}, u32[]{:S(2)}, u32[]{:S(2)}) collective-permute-start(bf16[128,2048]{1,0:T(8,128)(2,1)} %bitcast.5), channel_id=1, source_target_pairs={{0,24},{4,28},{8,16},{12,20},{16,8},{20,12},{24,0},{28,4},{1,25},{... | collective-permute-start | bytes 1572872 | tf_op jit(solution)/shard_map/ppermute | solution.py:440
  23.7 1.4 collective-permute-start.9
  25.2 2.5 %collective-permute-start.8 = (bf16[2,64,2048]{2,1,0:T(8,128)(2,1)}, bf16[2,64,2048]{2,1,0:T(8,128)(2,1)S(1)}, u32[]{:S(2)}, u32[]{:S(2)}) collective-permute-start(bf16[2,64,2048]{2,1,0:T(8,128)(2,1)} %get-tuple-element.46), channel_id=1, source_target_pairs={{0,24},{4,28},{8,16},{12,20},{16,8},{20,12},{24,0},{28,4},{1,25},{... | collective-permute-start | bytes 1572872 | tf_op jit(solution)/shard_map/ppermute | solution.py:440
  29.7 6.9 %collective-permute-done.10.refs_1_ = bf16[128,2048]{1,0:T(8,128)(2,1)S(1)} collective-permute-done((bf16[128,2048]{1,0:T(8,128)(2,1)}, bf16[128,2048]{1,0:T(8,128)(2,1)S(1)}, u32[]{:S(2)}, u32[]{:S(2)}) %collective-permute-start.10) | collective-permute-done | bytes 524320 | tf_op jit(solution)/shard_map/ppermute | solution.py:440
  36.6 0.8 copy-done.30
  37.4 1.5 collective-permute-start.29
  38.9 8.9 %collective-permute-done.9.refs_0_ = bf16[128,2048]{1,0:T(8,128)(2,1)S(1)} collective-permute-done((bf16[128,2048]{1,0:T(8,128)(2,1)}, bf16[128,2048]{1,0:T(8,128)(2,1)S(1)}, u32[]{:S(2)}, u32[]{:S(2)}) %collective-permute-start.9) | collective-permute-done | bytes 524320 | tf_op jit(solution)/shard_map/ppermute | solution.py:440
  47.8 1.5 collective-permute-start.30
  49.3 7.1 %collective-permute-done.8.refs_0_ = bf16[2,64,2048]{2,1,0:T(8,128)(2,1)S(1)} collective-permute-done((bf16[2,64,2048]{2,1,0:T(8,128)(2,1)}, bf16[2,64,2048]{2,1,0:T(8,128)(2,1)S(1)}, u32[]{:S(2)}, u32[]{:S(2)}) %collective-permute-start.8) | collective-permute-done | bytes 524320 | tf_op jit(solution)/shard_map/ppermute | solution.py:440
  56.4 35.2 %collective-permute-start.27 = (bf16[2,64,2048]{2,1,0:T(8,128)(2,1)}, bf16[2,64,2048]{2,1,0:T(8,128)(2,1)S(1)}, u32[]{:S(2)}, u32[]{:S(2)}) collective-permute-start(bf16[2,64,2048]{2,1,0:T(8,128)(2,1)} %get-tuple-element.46), channel_id=1, source_target_pairs={{0,8},{4,12},{24,16},{28,20},{1,9},{5,13},{25,17},{29,21},{2,10},{... | collective-permute-start | bytes 1572872 | tf_op jit(solution)/shard_map/ppermute | solution.py:443
  91.7 2.5 %collective-permute-start.1 = (bf16[2,64,2048]{2,1,0:T(8,128)(2,1)S(1)}, bf16[2,64,2048]{2,1,0:T(8,128)(2,1)S(1)}, u32[]{:S(2)}, u32[]{:S(2)}) collective-permute-start(bf16[2,64,2048]{2,1,0:T(8,128)(2,1)S(1)} %copy-done.43), channel_id=1, source_target_pairs={{0,24},{4,28},{8,16},{12,20},{16,8},{20,12},{24,0},{28,4},{1,25},{... | collective-permute-start | bytes 1572872 | tf_op jit(solution)/shard_map/ppermute | solution.py:440
  94.3 1.0 copy-done.31
  95.3 21.0 %attention.3 = (f32[256,256]{1,0:T(8,128)S(1)}, f32[256,256]{1,0:T(8,128)S(1)}, bf16[32,4096]{1,0:T(8,128)(2,1)S(1)}, bf16[32,4096]{1,0:T(8,128)(2,1)}, bf16[32,...) custom-call(s32[2]{0:T(128)S(1)} %pad_add_fusion.2.scal_ref, bf16[128,2048]{1,0:T(8,128)(2,1)S(1)} %collective-permute-done.9.refs_0_, ...), custom_call_target="tpu_custom_call" | custom-call | flops 16106127360 | bytes 20185088 | tf_op jit(solution)/shard_map/attention/pallas_call | solution.py:209
  116.3 0.7 copy-done.34
  117.1 0.7 copy-done.35
  117.8 0.8 copy-done.13
  118.6 1.3 collective-permute-start.25
  121.0 1.0 copy-done.33
  122.1 14.0 %attention.4 = (f32[256,256]{1,0:T(8,128)S(1)}, f32[256,256]{1,0:T(8,128)S(1)}, bf16[16,4096]{1,0:T(8,128)(2,1)S(1)}, bf16[16,4096]{1,0:T(8,128)(2,1)}, bf16[16,...) custom-call(s32[2]{0:T(128)S(1)} %pad_add_fusion.2.scal_ref, bf16[2,64,2048]{2,1,0:T(8,128)(2,1)S(1)} %copy-done.33, ...), custom_call_target="tpu_custom_call" | custom-call | flops 8053063680 | bytes 19136512 | tf_op jit(solution)/shard_map/attention/pallas_call | solution.py:209
  136.1 1.5 collective-permute-start.26
  137.6 13.9 %attention.5 = (f32[256,256]{1,0:T(8,128)S(1)}, f32[256,256]{1,0:T(8,128)S(1)}, bf16[16,4096]{1,0:T(8,128)(2,1)S(1)}, bf16[16,4096]{1,0:T(8,128)(2,1)S(1)}, bf16...) custom-call(s32[2]{0:T(128)S(1)} %pad_add_fusion.2.scal_ref, bf16[2,64,2048]{2,1,0:T(8,128)(2,1)S(1)} %collective-permute-done.1.refs_0_, ...), custom_call_target="tpu_custom_call" | custom-call | flops 8053063680 | bytes 19136512 | tf_op jit(solution)/shard_map/attention/pallas_call | solution.py:209
  151.5 0.7 copy-done.19
  152.8 0.8 copy-done.17
  154.0 1.0 copy-done.3
  155.0 1.0 copy-done.5
  156.0 2.6 %collective-permute-start.23 = (bf16[16,4096]{1,0:T(8,128)(2,1)S(1)}, bf16[16,4096]{1,0:T(8,128)(2,1)S(1)}, u32[]{:S(2)}, u32[]{:S(2)}) collective-permute-start(bf16[16,4096]{1,0:T(8,128)(2,1)S(1)} %get-tuple-element.70), channel_id=1, source_target_pairs={{0,2},{1,3},{2,0},{3,1},{4,6},{5,7},{6,4},{7,5},{8,10},{9,11},{10,... | collective-permute-start | bytes 393224 | tf_op jit(solution)/shard_map/ppermute | solution.py:507
  158.6 1.0 copy-done.7
  159.6 2.0 collective-permute-start.16
  161.6 1.0 copy-done.9
  163.3 1.5 collective-permute-start.19
  164.7 0.7 copy-done.24
  165.4 2.0 collective-permute-start.20
  167.4 0.7 copy-done.39
  168.2 1.9 share.1
  170.0 1.7 collective-permute-done.24.refs_15_
  171.8 1.6 collective-permute-start.17
  173.4 1.3 collective-permute-done.19.refs_9_
  174.7 1.5 collective-permute-start.18
  177.3 0.9 collective-permute-start.14
  178.3 2.0 collective-permute-start.15
  180.3 8.2 %collective-permute-done.17.refs_6_ = bf16[32,4096]{1,0:T(8,128)(2,1)S(1)} collective-permute-done((bf16[32,4096]{1,0:T(8,128)(2,1)}, bf16[32,4096]{1,0:T(8,128)(2,1)S(1)}, u32[]{:S(2)}, u32[]{:S(2)}) %collective-permute-start.17) | collective-permute-done | bytes 262176 | tf_op jit(solution)/shard_map/ppermute | solution.py:507
  188.8 1.2 copy-done.2
  190.0 1.2 copy-done.4
  191.2 1.2 copy-done.6
  192.5 1.2 copy-done.8
  193.7 1.2 copy-done.10
  194.9 1.0 copy-done.11
  195.9 1.0 copy-done.12
  197.0 1.0 copy-done.14
  198.0 1.0 copy-done.16
  199.1 1.0 copy-done.18
  200.1 0.9 copy-done.21
  201.0 0.9 copy-done.23
  201.9 0.9 copy-done.25
  202.8 0.8 copy-done.26
  203.6 0.7 copy-done.28
  204.2 6.4 %finish.1 = bf16[64,4096]{1,0:T(8,128)(2,1)} custom-call(s32[2]{0:T(128)S(1)} %copy-done.28, bf16[1,4096]{1,0:T(2,128)(2,1)S(1)} %broadcast_select_fusion.gain_ref, bf16[64,4096]{1,0:T(8,128)(2,1)S(1)} %copy-done.11, bf16[64,4096]{1,0:T(8,128)(2,1)S(1)} %copy-done.12, bf16[64,256]{1,0:T(8,128)(2,1)S(1)} %copy-done.26, ...), custom_call_target="tpu_custom_call" | custom-call | flops 1073741824 | bytes 8388608 | tf_op jit(solution)/shard_map/finish/pallas_call | solution.py:358
  (126 shorter events, 7.7 us)
Async XLA Ops:
  0.0 2.0 copy-start.36
  2.8 4.3 %copy-start.37 = (bf16[320,512]{1,0:T(8,128)(2,1)S(1)}, bf16[320,512]{1,0:T(8,128)(2,1)}, u32[]{:S(2)}) copy-start(bf16[320,512]{1,0:T(8,128)(2,1)} %param.16) | copy-start | bytes 983044
  2.8 4.3 %copy-start.38 = (bf16[320,512]{1,0:T(8,128)(2,1)S(1)}, bf16[320,512]{1,0:T(8,128)(2,1)}, u32[]{:S(2)}) copy-start(bf16[320,512]{1,0:T(8,128)(2,1)} %param.17) | copy-start | bytes 983044
  6.5 5.0 %copy-start.42 = (s32[256]{0:T(256)S(1)}, s32[256]{0:T(256)}, u32[]{:S(2)}) copy-start(s32[256]{0:T(256)} %param.19) | copy-start | bytes 3076
  6.5 8.5 %copy-start.41 = (s32[256]{0:T(256)S(1)}, s32[256]{0:T(256)}, u32[]{:S(2)}) copy-start(s32[256]{0:T(256)} %param.18) | copy-start | bytes 3076
  6.5 85.2 %collective-permute-start.11 = (bf16[2048,2048]{1,0:T(8,128)(2,1)}, bf16[2048,2048]{1,0:T(8,128)(2,1)}, u32[]{:S(2)}, u32[]{:S(2)}) collective-permute-start(bf16[2048,2048]{1,0:T(8,128)(2,1)} %refs_8_.1), channel_id=1, source_target_pairs={{0,4},{4,0},{8,12},{12,8},{16,20},{20,16},{24,28},{28,24},{1,5},{5... | collective-permute-start | bytes 25165832 | tf_op jit(solution)/shard_map/ppermute | solution.py:419
  7.2 20.8 %copy-start.40 = (bf16[2048]{0:T(1024)(128)(2,1)S(1)}, bf16[2048]{0:T(1024)(128)(2,1)}, u32[]{:S(2)}) copy-start(bf16[2048]{0:T(1024)(128)(2,1)} %param.23) | copy-start | bytes 12292
  7.3 7.6 %collective-permute-start.2 = (bf16[2,320,128]{2,1,0:T(8,128)(2,1)S(1)}, bf16[2,320,128]{2,1,0:T(8,128)(2,1)S(1)}, u32[]{:S(2)}, u32[]{:S(2)}) collective-permute-start(bf16[2,320,128]{2,1,0:T(8,128)(2,1)S(1)} %get-tuple-element.77), channel_id=1, source_target_pairs={{0,1},{1,0},{2,3},{3,2},{4,5},{5,4},{6,7},{7,6},{8,9},{9,8},{10,11... | collective-permute-start | bytes 491528 | tf_op jit(solution)/shard_map/ppermute | solution.py:452
  9.9 9.8 %collective-permute-start.3 = (bf16[2,320,128]{2,1,0:T(8,128)(2,1)S(1)}, bf16[2,320,128]{2,1,0:T(8,128)(2,1)S(1)}, u32[]{:S(2)}, u32[]{:S(2)}) collective-permute-start(bf16[2,320,128]{2,1,0:T(8,128)(2,1)S(1)} %get-tuple-element.78), channel_id=1, source_target_pairs={{0,2},{1,3},{2,0},{3,1},{4,6},{5,7},{6,4},{7,5},{8,10},{9,11},{10,... | collective-permute-start | bytes 491528 | tf_op jit(solution)/shard_map/ppermute | solution.py:452
  11.4 11.9 %collective-permute-start.4 = (bf16[2,320,128]{2,1,0:T(8,128)(2,1)S(1)}, bf16[2,320,128]{2,1,0:T(8,128)(2,1)S(1)}, u32[]{:S(2)}, u32[]{:S(2)}) collective-permute-start(bf16[2,320,128]{2,1,0:T(8,128)(2,1)S(1)} %get-tuple-element.75), channel_id=1, source_target_pairs={{0,3},{1,2},{2,1},{3,0},{4,7},{5,6},{6,5},{7,4},{8,11},{9,10},{10,... | collective-permute-start | bytes 491528 | tf_op jit(solution)/shard_map/ppermute | solution.py:452
  11.4 12.3 %collective-permute-start.7 = (s32[256]{0:T(256)S(1)}, s32[256]{0:T(256)S(1)}, u32[]{:S(2)}, u32[]{:S(2)}) collective-permute-start(s32[256]{0:T(256)S(1)} %copy-done.42), channel_id=1, source_target_pairs={{0,4},{4,0},{8,12},{12,8},{16,20},{20,16},{24,28},{28,24},{1,5},{5... | collective-permute-start | bytes 3080 | tf_op jit(solution)/shard_map/ppermute | solution.py:419
  15.0 10.2 %collective-permute-start.6 = (s32[256]{0:T(256)S(1)}, s32[256]{0:T(256)S(1)}, u32[]{:S(2)}, u32[]{:S(2)}) collective-permute-start(s32[256]{0:T(256)S(1)} %copy-done.41), channel_id=1, source_target_pairs={{0,4},{4,0},{8,12},{12,8},{16,20},{20,16},{24,28},{28,24},{1,5},{5... | collective-permute-start | bytes 3080 | tf_op jit(solution)/shard_map/ppermute | solution.py:419
  19.7 16.9 %collective-permute-start.10 = (bf16[128,2048]{1,0:T(8,128)(2,1)}, bf16[128,2048]{1,0:T(8,128)(2,1)S(1)}, u32[]{:S(2)}, u32[]{:S(2)}) collective-permute-start(bf16[128,2048]{1,0:T(8,128)(2,1)} %bitcast.5), channel_id=1, source_target_pairs={{0,24},{4,28},{8,16},{12,20},{16,8},{20,12},{24,0},{28,4},{1,25},{... | collective-permute-start | bytes 1572872 | tf_op jit(solution)/shard_map/ppermute | solution.py:440
  23.4 4.6 %collective-permute-start.5 = (bf16[2,1280,128]{2,1,0:T(8,128)(2,1)S(1)}, bf16[2,1280,128]{2,1,0:T(8,128)(2,1)S(1)}, u32[]{:S(2)}, u32[]{:S(2)}) collective-permute-start(bf16[2,1280,128]{2,1,0:T(8,128)(2,1)S(1)} %constant_dynamic-update-slice_fusion), channel_id=1, source_target_pairs={{0,4},{4,0},{8,12},{12,8},{16,20},{20,16},{24,28},{28,24},{1,5},{5... | collective-permute-start | bytes 1966088 | tf_op jit(solution)/shard_map/ppermute | solution.py:419
  23.5 114.0 %copy-start.27 = (s32[2]{0:T(128)}, s32[2]{0:T(128)S(1)}, u32[]{:S(2)}) copy-start(s32[2]{0:T(128)S(1)} %pad_add_fusion.2.scal_ref) | copy-start | bytes 28
  23.7 24.1 %collective-permute-start.9 = (bf16[128,2048]{1,0:T(8,128)(2,1)}, bf16[128,2048]{1,0:T(8,128)(2,1)S(1)}, u32[]{:S(2)}, u32[]{:S(2)}) collective-permute-start(bf16[128,2048]{1,0:T(8,128)(2,1)} %bitcast.3), channel_id=1, source_target_pairs={{0,24},{4,28},{8,16},{12,20},{16,8},{20,12},{24,0},{28,4},{1,25},{... | collective-permute-start | bytes 1572872 | tf_op jit(solution)/shard_map/ppermute | solution.py:440
  25.2 31.2 %collective-permute-start.8 = (bf16[2,64,2048]{2,1,0:T(8,128)(2,1)}, bf16[2,64,2048]{2,1,0:T(8,128)(2,1)S(1)}, u32[]{:S(2)}, u32[]{:S(2)}) collective-permute-start(bf16[2,64,2048]{2,1,0:T(8,128)(2,1)} %get-tuple-element.46), channel_id=1, source_target_pairs={{0,24},{4,28},{8,16},{12,20},{16,8},{20,12},{24,0},{28,4},{1,25},{... | collective-permute-start | bytes 1572872 | tf_op jit(solution)/shard_map/ppermute | solution.py:440
  28.0 1.2 collective-permute-start
  28.4 1.2 copy-start
  28.4 63.2 %copy-start.43 = (bf16[2,64,2048]{2,1,0:T(8,128)(2,1)S(1)}, bf16[2,64,2048]{2,1,0:T(8,128)(2,1)}, u32[]{:S(2)}) copy-start(bf16[2,64,2048]{2,1,0:T(8,128)(2,1)} %get-tuple-element.43) | copy-start | bytes 1572868
  28.5 65.8 %copy-start.29 = (bf16[256,2048]{1,0:T(8,128)(2,1)S(1)}, bf16[256,2048]{1,0:T(8,128)(2,1)}, u32[]{:S(2)}) copy-start(bf16[256,2048]{1,0:T(8,128)(2,1)} %param.13) | copy-start | bytes 3145732
  29.6 90.3 %collective-permute-start.28 = (bf16[2048,256]{1,0:T(8,128)(2,1)S(1)}, bf16[2048,256]{1,0:T(8,128)(2,1)S(1)}, u32[]{:S(2)}, u32[]{:S(2)}) collective-permute-start(bf16[2048,256]{1,0:T(8,128)(2,1)S(1)} %copy-done), channel_id=1, source_target_pairs={{0,1},{1,0},{2,3},{3,2},{4,5},{5,4},{6,7},{7,6},{8,9},{9,8},{10,11... | collective-permute-start | bytes 3145736 | tf_op jit(solution)/shard_map/ppermute | solution.py:481
  37.4 83.1 %collective-permute-start.29 = (bf16[2048,256]{1,0:T(8,128)(2,1)S(1)}, bf16[2048,256]{1,0:T(8,128)(2,1)S(1)}, u32[]{:S(2)}, u32[]{:S(2)}) collective-permute-start(bf16[2048,256]{1,0:T(8,128)(2,1)S(1)} %copy-done), channel_id=1, source_target_pairs={{0,2},{1,3},{2,0},{3,1},{4,6},{5,7},{6,4},{7,5},{8,10},{9,11},{10,... | collective-permute-start | bytes 3145736 | tf_op jit(solution)/shard_map/ppermute | solution.py:481
  47.8 72.8 %collective-permute-start.30 = (bf16[2048,256]{1,0:T(8,128)(2,1)S(1)}, bf16[2048,256]{1,0:T(8,128)(2,1)S(1)}, u32[]{:S(2)}, u32[]{:S(2)}) collective-permute-start(bf16[2048,256]{1,0:T(8,128)(2,1)S(1)} %copy-done), channel_id=1, source_target_pairs={{0,3},{1,2},{2,1},{3,0},{4,7},{5,6},{6,5},{7,4},{8,11},{9,10},{10,... | collective-permute-start | bytes 3145736 | tf_op jit(solution)/shard_map/ppermute | solution.py:481
  56.4 59.9 %copy-start.32 = (bf16[2,64,2048]{2,1,0:T(8,128)(2,1)}, bf16[2,64,2048]{2,1,0:T(8,128)(2,1)S(1)}, u32[]{:S(2)}) copy-start(bf16[2,64,2048]{2,1,0:T(8,128)(2,1)S(1)} %collective-permute-done.8.refs_0_) | copy-start | bytes 1572868
  56.4 61.4 %collective-permute-start.27 = (bf16[2,64,2048]{2,1,0:T(8,128)(2,1)}, bf16[2,64,2048]{2,1,0:T(8,128)(2,1)S(1)}, u32[]{:S(2)}, u32[]{:S(2)}) collective-permute-start(bf16[2,64,2048]{2,1,0:T(8,128)(2,1)} %get-tuple-element.46), channel_id=1, source_target_pairs={{0,8},{4,12},{24,16},{28,20},{1,9},{5,13},{25,17},{29,21},{2,10},{... | collective-permute-start | bytes 1572872 | tf_op jit(solution)/shard_map/ppermute | solution.py:443
  91.7 26.1 %collective-permute-start.1 = (bf16[2,64,2048]{2,1,0:T(8,128)(2,1)S(1)}, bf16[2,64,2048]{2,1,0:T(8,128)(2,1)S(1)}, u32[]{:S(2)}, u32[]{:S(2)}) collective-permute-start(bf16[2,64,2048]{2,1,0:T(8,128)(2,1)S(1)} %copy-done.43), channel_id=1, source_target_pairs={{0,24},{4,28},{8,16},{12,20},{16,8},{20,12},{24,0},{28,4},{1,25},{... | collective-permute-start | bytes 1572872 | tf_op jit(solution)/shard_map/ppermute | solution.py:440
  94.3 1.0 copy-start.31
  117.8 36.2 %collective-permute-start.31 = (bf16[2048,256]{1,0:T(8,128)(2,1)S(1)}, bf16[2048,256]{1,0:T(8,128)(2,1)S(1)}, u32[]{:S(2)}, u32[]{:S(2)}) collective-permute-start(bf16[2048,256]{1,0:T(8,128)(2,1)S(1)} %copy-done), channel_id=1, source_target_pairs={{0,4},{4,0},{8,12},{12,8},{16,20},{20,16},{24,28},{28,24},{1,5},{5... | collective-permute-start | bytes 3145736 | tf_op jit(solution)/shard_map/ppermute | solution.py:419
  118.6 17.4 %collective-permute-start.25 = (bf16[128,2048]{1,0:T(8,128)(2,1)}, bf16[128,2048]{1,0:T(8,128)(2,1)S(1)}, u32[]{:S(2)}, u32[]{:S(2)}) collective-permute-start(bf16[128,2048]{1,0:T(8,128)(2,1)} %bitcast.3), channel_id=1, source_target_pairs={{0,8},{4,12},{24,16},{28,20},{1,9},{5,13},{25,17},{29,21},{2,10},{... | collective-permute-start | bytes 1572872 | tf_op jit(solution)/shard_map/ppermute | solution.py:443
  119.9 35.1 %collective-permute-start.32 = (bf16[2048,256]{1,0:T(8,128)(2,1)S(1)}, bf16[2048,256]{1,0:T(8,128)(2,1)S(1)}, u32[]{:S(2)}, u32[]{:S(2)}) collective-permute-start(bf16[2048,256]{1,0:T(8,128)(2,1)S(1)} %collective-permute-done.28.refs_20_), channel_id=1, source_target_pairs={{0,4},{4,0},{8,12},{12,8},{16,20},{20,16},{24,28},{28,24},{1,5},{5... | collective-permute-start | bytes 3145736 | tf_op jit(solution)/shard_map/ppermute | solution.py:419
  120.5 38.1 %collective-permute-start.33 = (bf16[2048,256]{1,0:T(8,128)(2,1)S(1)}, bf16[2048,256]{1,0:T(8,128)(2,1)S(1)}, u32[]{:S(2)}, u32[]{:S(2)}) collective-permute-start(bf16[2048,256]{1,0:T(8,128)(2,1)S(1)} %collective-permute-done.29.refs_21_), channel_id=1, source_target_pairs={{0,4},{4,0},{8,12},{12,8},{16,20},{20,16},{24,28},{28,24},{1,5},{5... | collective-permute-start | bytes 3145736 | tf_op jit(solution)/shard_map/ppermute | solution.py:419
  120.6 15.4 %copy-start.1 = (bf16[2048,256]{1,0:T(8,128)(2,1)}, bf16[2048,256]{1,0:T(8,128)(2,1)S(1)}, u32[]{:S(2)}) copy-start(bf16[2048,256]{1,0:T(8,128)(2,1)S(1)} %collective-permute-done.30.refs_22_) | copy-start | bytes 3145732
  120.6 41.0 %collective-permute-start.34 = (bf16[2048,256]{1,0:T(8,128)(2,1)S(1)}, bf16[2048,256]{1,0:T(8,128)(2,1)S(1)}, u32[]{:S(2)}, u32[]{:S(2)}) collective-permute-start(bf16[2048,256]{1,0:T(8,128)(2,1)S(1)} %collective-permute-done.30.refs_22_), channel_id=1, source_target_pairs={{0,4},{4,0},{8,12},{12,8},{16,20},{20,16},{24,28},{28,24},{1,5},{5... | collective-permute-start | bytes 3145736 | tf_op jit(solution)/shard_map/ppermute | solution.py:419
  121.0 1.0 copy-start.33
  136.0 15.4 %copy-start.15 = (bf16[128,2048]{1,0:T(8,128)(2,1)}, bf16[128,2048]{1,0:T(8,128)(2,1)S(1)}, u32[]{:S(2)}) copy-start(bf16[128,2048]{1,0:T(8,128)(2,1)S(1)} %collective-permute-done.25.refs_16_) | copy-start | bytes 1572868
  136.1 16.8 %collective-permute-start.26 = (bf16[128,2048]{1,0:T(8,128)(2,1)}, bf16[128,2048]{1,0:T(8,128)(2,1)S(1)}, u32[]{:S(2)}, u32[]{:S(2)}) collective-permute-start(bf16[128,2048]{1,0:T(8,128)(2,1)} %bitcast.5), channel_id=1, source_target_pairs={{0,8},{4,12},{24,16},{28,20},{1,9},{5,13},{25,17},{29,21},{2,10},{... | collective-permute-start | bytes 1572872 | tf_op jit(solution)/shard_map/ppermute | solution.py:443
  153.6 13.8 %collective-permute-start.12 = (f32[256,256]{1,0:T(8,128)S(1)}, f32[256,256]{1,0:T(8,128)S(1)}, u32[]{:S(2)}, u32[]{:S(2)}) collective-permute-start(f32[256,256]{1,0:T(8,128)S(1)} %get-tuple-element.55), channel_id=1, source_target_pairs={{0,4},{4,0},{8,12},{12,8},{16,20},{20,16},{24,28},{28,24},{1,5},{5... | collective-permute-start | bytes 786440 | tf_op jit(solution)/shard_map/ppermute | solution.py:419
  154.0 1.0 copy-start.3
  155.0 7.6 %collective-permute-start.22 = (bf16[16,4096]{1,0:T(8,128)(2,1)S(1)}, bf16[16,4096]{1,0:T(8,128)(2,1)S(1)}, u32[]{:S(2)}, u32[]{:S(2)}) collective-permute-start(bf16[16,4096]{1,0:T(8,128)(2,1)S(1)} %get-tuple-element.69), channel_id=1, source_target_pairs={{0,1},{1,0},{2,3},{3,2},{4,5},{5,4},{6,7},{7,6},{8,9},{9,8},{10,11... | collective-permute-start | bytes 393224 | tf_op jit(solution)/shard_map/ppermute | solution.py:507
  155.0 1.0 copy-start.5
  156.0 8.7 %collective-permute-start.23 = (bf16[16,4096]{1,0:T(8,128)(2,1)S(1)}, bf16[16,4096]{1,0:T(8,128)(2,1)S(1)}, u32[]{:S(2)}, u32[]{:S(2)}) collective-permute-start(bf16[16,4096]{1,0:T(8,128)(2,1)S(1)} %get-tuple-element.70), channel_id=1, source_target_pairs={{0,2},{1,3},{2,0},{3,1},{4,6},{5,7},{6,4},{7,5},{8,10},{9,11},{10,... | collective-permute-start | bytes 393224 | tf_op jit(solution)/shard_map/ppermute | solution.py:507
  158.6 1.0 copy-start.7
  159.6 18.7 %collective-permute-start.16 = (bf16[32,4096]{1,0:T(8,128)(2,1)}, bf16[32,4096]{1,0:T(8,128)(2,1)}, u32[]{:S(2)}, u32[]{:S(2)}) collective-permute-start(bf16[32,4096]{1,0:T(8,128)(2,1)} %get-tuple-element.61), channel_id=1, source_target_pairs={{0,1},{1,0},{2,3},{3,2},{4,5},{5,4},{6,7},{7,6},{8,9},{9,8},{10,11... | collective-permute-start | bytes 786440 | tf_op jit(solution)/shard_map/ppermute | solution.py:507
  161.6 1.0 copy-start.9
  162.6 9.2 %collective-permute-start.24 = (bf16[16,4096]{1,0:T(8,128)(2,1)}, bf16[16,4096]{1,0:T(8,128)(2,1)}, u32[]{:S(2)}, u32[]{:S(2)}) collective-permute-start(bf16[16,4096]{1,0:T(8,128)(2,1)} %get-tuple-element.71), channel_id=1, source_target_pairs={{0,3},{1,2},{2,1},{3,0},{4,7},{5,6},{6,5},{7,4},{8,11},{9,10},{10,... | collective-permute-start | bytes 393224 | tf_op jit(solution)/shard_map/ppermute | solution.py:507
  163.3 11.4 %collective-permute-start.19 = (bf16[16,4096]{1,0:T(8,128)(2,1)}, bf16[16,4096]{1,0:T(8,128)(2,1)}, u32[]{:S(2)}, u32[]{:S(2)}) collective-permute-start(bf16[16,4096]{1,0:T(8,128)(2,1)} %get-tuple-element.65), channel_id=1, source_target_pairs={{0,1},{1,0},{2,3},{3,2},{4,5},{5,4},{6,7},{7,6},{8,9},{9,8},{10,11... | collective-permute-start | bytes 393224 | tf_op jit(solution)/shard_map/ppermute | solution.py:507
  165.4 10.8 %collective-permute-start.20 = (bf16[16,4096]{1,0:T(8,128)(2,1)}, bf16[16,4096]{1,0:T(8,128)(2,1)}, u32[]{:S(2)}, u32[]{:S(2)}) collective-permute-start(bf16[16,4096]{1,0:T(8,128)(2,1)} %get-tuple-element.66), channel_id=1, source_target_pairs={{0,2},{1,3},{2,0},{3,1},{4,6},{5,7},{6,4},{7,5},{8,10},{9,11},{10,... | collective-permute-start | bytes 393224 | tf_op jit(solution)/shard_map/ppermute | solution.py:507
  168.1 9.2 %collective-permute-start.21 = (bf16[16,4096]{1,0:T(8,128)(2,1)}, bf16[16,4096]{1,0:T(8,128)(2,1)}, u32[]{:S(2)}, u32[]{:S(2)}) collective-permute-start(bf16[16,4096]{1,0:T(8,128)(2,1)} %get-tuple-element.67), channel_id=1, source_target_pairs={{0,3},{1,2},{2,1},{3,0},{4,7},{5,6},{6,5},{7,4},{8,11},{9,10},{10,... | collective-permute-start | bytes 393224 | tf_op jit(solution)/shard_map/ppermute | solution.py:507
  171.8 16.7 %collective-permute-start.17 = (bf16[32,4096]{1,0:T(8,128)(2,1)}, bf16[32,4096]{1,0:T(8,128)(2,1)S(1)}, u32[]{:S(2)}, u32[]{:S(2)}) collective-permute-start(bf16[32,4096]{1,0:T(8,128)(2,1)} %copy-done.35), channel_id=1, source_target_pairs={{0,2},{1,3},{2,0},{3,1},{4,6},{5,7},{6,4},{7,5},{8,10},{9,11},{10,... | collective-permute-start | bytes 786440 | tf_op jit(solution)/shard_map/ppermute | solution.py:507
  174.7 13.7 %collective-permute-start.18 = (bf16[32,4096]{1,0:T(8,128)(2,1)}, bf16[32,4096]{1,0:T(8,128)(2,1)S(1)}, u32[]{:S(2)}, u32[]{:S(2)}) collective-permute-start(bf16[32,4096]{1,0:T(8,128)(2,1)} %copy-done.34), channel_id=1, source_target_pairs={{0,3},{1,2},{2,1},{3,0},{4,7},{5,6},{6,5},{7,4},{8,11},{9,10},{10,... | collective-permute-start | bytes 786440 | tf_op jit(solution)/shard_map/ppermute | solution.py:507
  176.2 12.3 %collective-permute-start.13 = (bf16[64,256]{1,0:T(8,128)(2,1)}, bf16[64,256]{1,0:T(8,128)(2,1)S(1)}, u32[]{:S(2)}, u32[]{:S(2)}) collective-permute-start(bf16[64,256]{1,0:T(8,128)(2,1)} %get-tuple-element.57), channel_id=1, source_target_pairs={{0,1},{1,0},{2,3},{3,2},{4,5},{5,4},{6,7},{7,6},{8,9},{9,8},{10,11... | collective-permute-start | bytes 98312 | tf_op jit(solution)/shard_map/ppermute | solution.py:512
  177.3 11.5 %collective-permute-start.14 = (bf16[64,256]{1,0:T(8,128)(2,1)}, bf16[64,256]{1,0:T(8,128)(2,1)S(1)}, u32[]{:S(2)}, u32[]{:S(2)}) collective-permute-start(bf16[64,256]{1,0:T(8,128)(2,1)} %get-tuple-element.58), channel_id=1, source_target_pairs={{0,2},{1,3},{2,0},{3,1},{4,6},{5,7},{6,4},{7,5},{8,10},{9,11},{10,... | collective-permute-start | bytes 98312 | tf_op jit(solution)/shard_map/ppermute | solution.py:512
  178.3 10.5 %collective-permute-start.15 = (bf16[64,256]{1,0:T(8,128)(2,1)}, bf16[64,256]{1,0:T(8,128)(2,1)S(1)}, u32[]{:S(2)}, u32[]{:S(2)}) collective-permute-start(bf16[64,256]{1,0:T(8,128)(2,1)} %get-tuple-element.59), channel_id=1, source_target_pairs={{0,3},{1,2},{2,1},{3,0},{4,7},{5,6},{6,5},{7,4},{8,11},{9,10},{10,... | collective-permute-start | bytes 98312 | tf_op jit(solution)/shard_map/ppermute | solution.py:512
  188.8 1.2 copy-start.2
  190.0 1.2 copy-start.4
  191.2 1.2 copy-start.6
  192.5 1.2 copy-start.8
  193.7 1.2 copy-start.10
  194.9 1.0 copy-start.11
  195.9 1.0 copy-start.12
  197.0 1.0 copy-start.14
  198.0 1.0 copy-start.16
  199.1 1.0 copy-start.18
  (15 other events, 11.4 us)

commit v2 on v1

v2 whole, which is shorter than its diff:
```python
import functools
import math

import jax
import jax.numpy as jnp
from jax import lax
from jax.experimental import pallas as pl
from jax.experimental.pallas import tpu as pltpu
from jax.sharding import PartitionSpec as P


KVH = 4
HD = 128
SL = 256
CTX = 2048
REACH = 128

epsilon = 1e-06
far_negative = -1e30
factor = 1.0 / math.sqrt(HD)
log2_factor = factor * math.log2(math.e)

CHUNK_EIGHTHS = (4, 2, 2)
ROW_BLOCK = 512
KEY_BLOCK = 512
FEATURE_TILE = 1024
VMEM_LIMIT = 46 * 2**20
LAST_VMEM_LIMIT = 46 * 2**20


NT = (((1,), (1,)), ((), ()))
TN = (((0,), (0,)), ((), ()))
NN = (((1,), (0,)), ((), ()))


def dot(left, right, dims):
    return lax.dot_general(left, right, dims, preferred_element_type=jnp.float32)


def xor_pairs(axis, mask):
    return [(i, i ^ mask) for i in range(lax.axis_size(axis))]


def inward_pairs(section_count):
    if section_count != 8:
        return []
    return [(0, 2), (1, 3), (6, 4), (7, 5)]


def chunk_plan(group_tokens):
    if group_tokens % 64:
        half = group_tokens // 2
        return [(0, half), (half, group_tokens - half)]
    plan, start = [], 0
    for eighths in CHUNK_EIGHTHS:
        count = group_tokens * eighths // 8
        plan.append((start, count))
        start += count
    return plan


def flush_points(plan):
    return {max(0, len(plan) - 2), len(plan) - 1}


def lane_tiles(values):
    return [values[:, j * HD:(j + 1) * HD] for j in range(values.shape[1] // HD)]


def fold(op, tiles):
    out = tiles[0]
    for tile in tiles[1:]:
        out = op(out, tile)
    return out


def attention_kernel(
    *refs, tokens, local_heads, head_count, paired, first, before, flush, grad_start
):
    if paired:
        q_ref, o_ref, refs = refs[0].at[0], refs[0].at[1], refs[1:]
    else:
        q_ref, o_ref, refs = refs[0], refs[1], refs[2:]
    g_ref, pair_ref, bias_c_ref, bias_s_ref, refs = *refs[:4], refs[4:]
    prev_refs, refs = ((), refs) if first else (refs[:2], refs[2:])
    dq_before, refs = refs[:len(before)], refs[len(before):]
    weight_refs, refs = (refs[:2], refs[2:]) if flush else ((), refs)
    kv_refs, refs = refs[:2], refs[2:]
    parity, head = lax.axis_index("section") % 2, lax.axis_index("head")
    heads = min(local_heads, max(1, ROW_BLOCK // tokens))
    blocks = local_heads // heads
    cache_blocks = CTX // KEY_BLOCK
    held = sum(before)
    if flush:
        outs, refs = refs[:head_count], refs[head_count:]
        s_ref, dq_ref, weights, groups, sems = refs
        half, tile = weights.shape[2], groups.shape[2]

        def weight_copy(side):
            return pltpu.make_async_copy(weight_refs[side], weights.at[side], sems.at[side])

        for side in range(2):
            weight_copy(side).start()
        row = 0
        for ref, rows in zip(dq_before, before):
            dq_ref[row:row + rows, :] = ref[...]
            row += rows
        dq_ref = dq_ref.at[held:]
    else:
        dq_ref, s_ref = refs
    for index, ref in enumerate(kv_refs):
        ref[...] = jnp.zeros_like(ref) if first else prev_refs[index][...]
    slice_parts = [
        (0, SL, pl.multiple_of(CTX + parity * SL, SL)),
        (SL, REACH, pl.multiple_of(CTX + SL - parity * REACH, REACH)),
    ]

    def block(index, carry):
        def rows_of(ref):
            parts = []
            for j in range(heads):
                lanes = pl.ds(pl.multiple_of((index * heads + j) * HD, HD), HD)
                part = ref[..., lanes]
                if part.size != tokens * HD:
                    part = part.astype(jnp.float32)[:, grad_start:grad_start + tokens // head_count]
                parts.append(part.reshape(tokens, HD).astype(jnp.bfloat16))
            return parts[0] if heads == 1 else jnp.concatenate(parts, axis=0)

        q_rows, g_rows = rows_of(q_ref), rows_of(g_ref)
        delta = jnp.sum(
            g_rows.astype(jnp.float32) * rows_of(o_ref).astype(jnp.float32), axis=1, keepdims=True
        )
        running = None
        for kb in range(cache_blocks):
            keys = slice(kb * KEY_BLOCK, (kb + 1) * KEY_BLOCK)
            scores = dot(q_rows, pair_ref[0, keys, :], NT)
            if (kb + 1) * KEY_BLOCK > CTX // 2:
                scores = scores + bias_c_ref[:, keys]
            s_ref[:, keys] = scores
            top = fold(jnp.maximum, lane_tiles(scores))
            running = top if running is None else jnp.maximum(running, top)
        bias = bias_s_ref[...].reshape(tokens, bias_s_ref.shape[-1])
        bias = bias if heads == 1 else jnp.concatenate([bias] * heads, axis=0)
        for lane, count, row in slice_parts:
            scores = dot(q_rows, pair_ref[0, pl.ds(row, count), :], NT) + bias[:, lane:lane + count]
            s_ref[:, CTX + lane:CTX + lane + count] = scores
            running = jnp.maximum(running, fold(jnp.maximum, lane_tiles(scores)))
        shift = jnp.max(running, axis=1, keepdims=True) * log2_factor

        total = None
        query_grad = None
        for kb in range(cache_blocks):
            keys = slice(kb * KEY_BLOCK, (kb + 1) * KEY_BLOCK)
            probs = jnp.exp2(s_ref[:, keys] * log2_factor - shift)
            part = fold(jnp.add, lane_tiles(probs))
            total = part if total is None else total + part
            prob_grad = dot(g_rows, pair_ref[1, keys, :], NT)
            score_grad = (probs * (prob_grad - delta)).astype(jnp.bfloat16)
            term = dot(score_grad, pair_ref[0, keys, :], NN)
            query_grad = term if query_grad is None else query_grad + term
        probs = jnp.exp2(s_ref[:, CTX:] * log2_factor - shift)
        total = total + fold(jnp.add, lane_tiles(probs))
        scale = 1.0 / jnp.sum(total, axis=1, keepdims=True)
        probs = probs * scale
        query_grad = query_grad * (scale * factor)
        for part, (lane, count, row) in enumerate(slice_parts):
            rows = pl.ds(row, count)
            part_probs = probs[:, lane:lane + count]
            prob_grad = dot(g_rows, pair_ref[1, rows, :], NT)
            score_grad = (part_probs * (prob_grad - delta) * factor).astype(jnp.bfloat16)
            query_grad = query_grad + dot(score_grad, pair_ref[0, rows, :], NN)
            kv_refs[part][:HD, :] += dot(q_rows, score_grad, TN)
            kv_refs[part][HD:, :] += dot(g_rows, part_probs.astype(jnp.bfloat16), TN)
        query_grad = query_grad.astype(jnp.bfloat16)
        for j in range(heads):
            dq_ref[:, pl.ds(pl.multiple_of((index * heads + j) * HD, HD), HD)] = query_grad[
                j * tokens:(j + 1) * tokens
            ]
        return carry

    lax.fori_loop(0, blocks, block, 0)
    if not flush:
        return

    all_rows = refs[1]
    spans, row, place = [], 0, 0
    for rows in (*before, tokens):
        spans.append((row, place, rows // head_count))
        row, place = row + rows, place + rows // head_count
    for side in range(2):
        weight_copy(side).wait()
        column = parity if side == 0 else 1 - parity

        def project(index, carry):
            source = pl.ds(pl.multiple_of(index * tile, tile), tile)
            result = dot(all_rows[...], weights[side, :, source], NN)
            for row, place, count in spans:
                for group in range(head_count):
                    start = row + group * count
                    groups[group, place:place + count] = result[start:start + count]
            lanes = pl.ds(pl.multiple_of(column * half + index * tile, tile), tile)
            for d, out in enumerate(outs):
                out[:, lanes] = groups[head ^ d].astype(jnp.bfloat16)
            return carry

        lax.fori_loop(0, half // tile, project, 0)


def whole_block(array):
    return pl.BlockSpec(array.shape, lambda step: (0,) * array.ndim)


def token_block(array, start, count, head_count, tile):
    width = array.shape[1]
    grouped = array.reshape(head_count, array.shape[0] // head_count, width)
    rows = max(count, tile)
    block = start // rows
    return (
        grouped,
        pl.BlockSpec((head_count, rows, width), lambda step: (0, block, 0)),
        start - block * rows,
    )


def attention(
    stash, grads, pair, bias_c, biases, prev, before, weights, head_count, vmem_limit
):
    tokens, width = stash[0].shape[-2:]
    local_heads = width // HD
    heads = min(local_heads, max(1, ROW_BLOCK // tokens))
    keys = CTX + SL + REACH
    flush = weights is not None
    operands = [(array, whole_block(array)) for array in stash]
    operands += [grads[:2]] + [(array, whole_block(array)) for array in (pair, bias_c)]
    operands += [biases[:2]]
    operands += [(array, whole_block(array)) for array in (*prev, *before)]
    results = [jax.ShapeDtypeStruct((2 * HD, count), jnp.float32) for count in (SL, REACH)]
    scratch = [pltpu.VMEM((heads * tokens, keys), jnp.float32)]
    cost = 3 * tokens * local_heads * keys * HD
    if flush:
        half = weights[0].shape[1]
        tile = min(half, FEATURE_TILE)
        rows = tokens + sum(array.shape[0] for array in before)
        count = rows // head_count
        operands += [(array, pl.BlockSpec(memory_space=pl.ANY)) for array in weights]
        results += [
            jax.ShapeDtypeStruct((count, 2 * half), jnp.bfloat16) for _ in range(head_count)
        ]
        scratch += [
            pltpu.VMEM((rows, width), jnp.bfloat16),
            pltpu.VMEM((2, width, half), jnp.bfloat16),
            pltpu.VMEM((head_count, count, tile), jnp.float32),
            pltpu.SemaphoreType.DMA((2,)),
        ]
        cost += 2 * rows * width * half
    else:
        results += [jax.ShapeDtypeStruct((tokens, width), jnp.bfloat16)]
    outs = pl.pallas_call(
        functools.partial(
            attention_kernel,
            tokens=tokens,
            local_heads=local_heads,
            head_count=head_count,
            paired=len(stash) == 1,
            first=not prev,
            before=tuple(array.shape[0] for array in before),
            flush=flush,
            grad_start=grads[2],
        ),
        out_shape=results,
        grid=(1,),
        in_specs=[spec for _, spec in operands],
        out_specs=[whole_block(result) for result in results],
        scratch_shapes=scratch,
        compiler_params=pltpu.CompilerParams(vmem_limit_bytes=vmem_limit),
        cost_estimate=pl.CostEstimate(
            flops=8 * cost,
            bytes_accessed=4 * tokens * width * 2 + keys * HD * 4,
            transcendentals=tokens * local_heads * keys,
        ),
        name="attention",
    )(*[array for array, _ in operands])
    return outs[:2], outs[2:]


def split_kernel(*refs, sharers):
    head = lax.axis_index("head")
    sources, outs = refs[:2], refs[2:]
    for d, out in enumerate(outs):
        lanes = pl.ds(pl.multiple_of((head ^ d) // sharers * HD, HD), HD)
        for index, source in enumerate(sources):
            out[index] = source[:, lanes]


def split_heads(arrays, head_count):
    rows = arrays[0].shape[0]
    results = [jax.ShapeDtypeStruct((2, rows, HD), arrays[0].dtype) for _ in range(head_count)]
    return pl.pallas_call(
        functools.partial(split_kernel, sharers=head_count // KVH),
        out_shape=results,
        grid=(1,),
        in_specs=[whole_block(array) for array in arrays],
        out_specs=[whole_block(result) for result in results],
        compiler_params=pltpu.CompilerParams(vmem_limit_bytes=VMEM_LIMIT),
        name="split",
    )(*arrays)


def arrange_kernel(*refs):
    pieces, out_ref = refs[:-1], refs[-1]
    parity, head = lax.axis_index("section") % 2, lax.axis_index("head")
    head_count = len(pieces) // 2
    rows = pieces[0].shape[1]
    for index, piece in enumerate(pieces):
        place = parity if index < head_count else 1 - parity
        start = (place * head_count + (head ^ index % head_count)) * rows
        out_ref[:, pl.ds(pl.multiple_of(start, 16), rows)] = piece[...]


def arrange(pieces):
    rows = pieces[0].shape[1]
    result = jax.ShapeDtypeStruct((2, len(pieces) * rows, HD), pieces[0].dtype)
    return pl.pallas_call(
        arrange_kernel,
        out_shape=result,
        grid=(1,),
        in_specs=[whole_block(piece) for piece in pieces],
        out_specs=whole_block(result),
        compiler_params=pltpu.CompilerParams(vmem_limit_bytes=VMEM_LIMIT),
        name="arrange",
    )(*pieces)


def pack_kernel(q_ref, o_ref, *outs, plan, group_tokens, head_count):
    for out, (start, count) in zip(outs, plan):
        for group in range(head_count):
            rows = slice(group * group_tokens + start, group * group_tokens + start + count)
            out[0, group * count:(group + 1) * count] = q_ref[rows]
            out[1, group * count:(group + 1) * count] = o_ref[rows]


def pack(q, o, plan, group_tokens, head_count):
    tokens, width = q.shape
    lanes = min(width, 512)
    return pl.pallas_call(
        functools.partial(
            pack_kernel, plan=plan, group_tokens=group_tokens, head_count=head_count
        ),
        out_shape=[
            jax.ShapeDtypeStruct((2, head_count * count, width), q.dtype) for _, count in plan
        ],
        grid=(width // lanes,),
        in_specs=[pl.BlockSpec((tokens, lanes), lambda step: (0, step))] * 2,
        out_specs=[
            pl.BlockSpec((2, head_count * count, lanes), lambda step: (0, 0, step))
            for _, count in plan
        ],
        name="pack",
    )(q, o)


def transpose_kernel(in_ref, out_ref):
    out_ref[...] = in_ref[...].T


def transposed(array):
    rows, columns = array.shape
    tile = math.gcd(rows, 512)
    return pl.pallas_call(
        transpose_kernel,
        out_shape=jax.ShapeDtypeStruct((columns, rows), array.dtype),
        grid=(rows // tile,),
        in_specs=[pl.BlockSpec((tile, columns), lambda step: (step, 0))],
        out_specs=pl.BlockSpec((columns, tile), lambda step: (0, step)),
        compiler_params=pltpu.CompilerParams(vmem_limit_bytes=VMEM_LIMIT),
        cost_estimate=pl.CostEstimate(
            flops=rows * columns, bytes_accessed=4 * rows * columns, transcendentals=0
        ),
        name="transposed",
    )(array)


def share_kernel(own_ref, recv_ref, *refs):
    outs, total_ref = refs[:-1], refs[-1]
    head = lax.axis_index("head")
    count = outs[0].shape[0]
    parity = lax.axis_index("section") % 2
    lanes = pl.ds(pl.multiple_of((1 - parity) * (SL - REACH), REACH), REACH)
    total_ref[...] = own_ref[...]
    total_ref[:, lanes] += recv_ref[...]
    total = total_ref[...].T
    head_count = len(outs)
    for d, out in enumerate(outs):
        for group in range(head_count):

            @pl.when((head ^ d) == group)
            def _():
                out[...] = total[group * count:(group + 1) * count].astype(out.dtype)


def share_kv(own, recv, head_count, dtype):
    width, tokens = own.shape
    count = tokens // head_count
    results = [jax.ShapeDtypeStruct((count, width), dtype) for _ in range(head_count)]
    return pl.pallas_call(
        share_kernel,
        out_shape=results,
        grid=(1,),
        in_specs=[whole_block(own), whole_block(recv)],
        out_specs=[whole_block(result) for result in results],
        scratch_shapes=[pltpu.VMEM(own.shape, jnp.float32)],
        compiler_params=pltpu.CompilerParams(vmem_limit_bytes=4*2**20),
        cost_estimate=pl.CostEstimate(
            flops=tokens * width, bytes_accessed=tokens * width * 10, transcendentals=0
        ),
        name="share",
    )(own, recv)


def finish_kernel(*refs, plan, head_count, spent):
    shares = len(plan) * head_count
    inputs = 3 + head_count + shares
    sources, refs = refs[:inputs], refs[inputs + spent:]
    weight_sources, refs = refs[:2 * head_count], refs[2 * head_count:]
    out_ref, refs = refs[0], refs[1:]
    locals_, refs = refs[:inputs], refs[inputs:]
    gathered, total_ref, input_sems = refs
    parity, head = lax.axis_index("section") % 2, lax.axis_index("head")
    sharers = head_count // KVH
    width, half = weight_sources[0].shape
    step = min(width, HD)

    def input_copy(index):
        return pltpu.make_async_copy(sources[index], locals_[index], input_sems.at[index])

    for index in range(inputs):
        input_copy(index).start()
    gain_ref, x_ref, res_ref = locals_[:3]
    kv_pieces, pieces = locals_[3:3 + head_count], locals_[3 + head_count:]
    for index in range(3, 3 + head_count):
        input_copy(index).wait()
    if sharers > 1:
        gathered[...] = jnp.zeros_like(gathered)
    for d, piece in enumerate(kv_pieces):
        group = (head ^ d) // sharers
        for part in range(2):
            column = group * HD + part * KVH * HD
            for lane in range(0, HD, step):
                place = (column + lane) // width
                lanes = pl.ds(pl.multiple_of((column + lane) % width, step), step)
                if step == width:
                    lanes = slice(0, width)
                value = piece[:, part * HD + lane:part * HD + lane + step].astype(jnp.float32)
                if sharers > 1:
                    value = gathered[place, :, lanes] + value
                gathered[place, :, lanes] = value
    for side in range(2):
        place = parity if side == 0 else 1 - parity
        lanes = pl.ds(pl.multiple_of(place * half, half), half)
        terms = []
        for d in range(head_count):
            left = gathered[head ^ d].astype(jnp.bfloat16)
            terms.append(dot(left, weight_sources[side * head_count + d][...], NN))
        total_ref[:, lanes] = fold(jnp.add, terms)
    for index in [*range(3), *range(3 + head_count, inputs)]:
        input_copy(index).wait()
    x = x_ref[...].astype(jnp.float32)
    inverse = lax.rsqrt(jnp.mean(x * x, axis=1, keepdims=True) + epsilon)
    for c, (start, count) in enumerate(plan):
        rows = slice(start, start + count)
        parts = [pieces[c * head_count + d][...].astype(jnp.float32) for d in range(head_count)]
        total = total_ref[rows, :] + fold(jnp.add, parts)
        total_ref[rows, :] = gain_ref[...].astype(jnp.float32) * total
    mean = jnp.mean(total_ref[...] * x_ref[...].astype(jnp.float32), axis=1, keepdims=True)
    mean = inverse * inverse * inverse * mean
    out_ref[...] = (
        res_ref[...].astype(jnp.float32)
        + inverse * total_ref[...]
        - x_ref[...].astype(jnp.float32) * mean
    ).astype(out_ref.dtype)


def finish(gain, x, residual, kv_pieces, pieces, spent, weights, plan):
    head_count = len(kv_pieces)
    width, half = weights[0].shape
    rows = x.shape[0]
    local = [gain, x, residual, *kv_pieces, *pieces]
    remote = [*spent, *weights]
    early = [pltpu.HBM] * (len(pieces) - head_count + 1)
    late = [pl.ANY] * (head_count - 1)
    spaces = [pltpu.HBM] * 3 + [pl.ANY] * head_count + early + late
    return pl.pallas_call(
        functools.partial(
            finish_kernel, plan=plan, head_count=head_count, spent=len(spent)
        ),
        out_shape=jax.ShapeDtypeStruct(x.shape, jnp.bfloat16),
        in_specs=[pl.BlockSpec(memory_space=space) for space in spaces]
        + [pl.BlockSpec(memory_space=pltpu.HBM) for _ in spent]
        + [pl.BlockSpec(memory_space=pltpu.VMEM) for _ in weights],
        out_specs=pl.BlockSpec(memory_space=pltpu.VMEM),
        scratch_shapes=[pltpu.VMEM(array.shape, array.dtype) for array in local]
        + [
            pltpu.VMEM((head_count, rows, width), jnp.float32),
            pltpu.VMEM((rows, 2 * half), jnp.float32),
            pltpu.SemaphoreType.DMA((len(local),)),
        ],
        compiler_params=pltpu.CompilerParams(vmem_limit_bytes=24*2**20),
        cost_estimate=pl.CostEstimate(
            flops=512 * half * width * head_count,
            bytes_accessed=4 * half * width * head_count,
            transcendentals=0,
        ),
        name="finish",
    )(*local, *remote)


def body(
    out_grad,
    held_query,
    held_output,
    key_cache,
    value_cache,
    segment_ids,
    image_flags,
    cache_length,
    query_weight,
    kv_weight,
    norm_gain,
    layer_input,
    residual_grad,
):
    head_count = lax.axis_size("head")
    section_count = lax.axis_size("section")
    parity = lax.axis_index("section") % 2
    is_first = parity == 0
    sharers = head_count // KVH
    group_tokens = SL // head_count
    plan = chunk_plan(group_tokens)

    def rows_of_chunk(array, start, count):
        grouped = array.reshape(head_count, group_tokens, array.shape[1])
        return grouped[:, start:start + count].reshape(head_count * count, array.shape[1])

    def swap_cores(value):
        return lax.ppermute(value, "section", xor_pairs("section", 1))

    def ordered(own_value, other_value, axis):
        return jnp.where(
            is_first,
            jnp.concatenate([own_value, other_value], axis),
            jnp.concatenate([other_value, own_value], axis),
        )

    mirror = xor_pairs("section", section_count - 2)
    inward = inward_pairs(section_count)
    first_query = rows_of_chunk(held_query, *plan[0])
    first_query, held_output = lax.optimization_barrier((first_query, held_output))
    first_output = rows_of_chunk(held_output, *plan[0])
    first = [first_query, first_output]
    first_output, held_query, held_output = lax.optimization_barrier(
        (first_output, held_query, held_output)
    )
    buffers = pack(held_query, held_output, plan[1:], group_tokens, head_count)
    buffers, (key_cache, value_cache, kv_weight, query_weight) = lax.optimization_barrier(
        (buffers, (key_cache, value_cache, kv_weight, query_weight))
    )
    stash, spent = [], []
    for c, group in enumerate([first] + [[buffer] for buffer in buffers]):
        stash.append([])
        for buffer in group:
            stash[-1].append(lax.ppermute(buffer, "section", mirror))
        if inward and c in (0, 1):
            spent.append(lax.ppermute(group[0] if c else held_query, "section", inward))

    other_segments = swap_cores(segment_ids)
    other_flags = swap_cores(image_flags)
    other_gain = swap_cores(norm_gain)
    gain = ordered(norm_gain, other_gain, 0)[None, :]

    split = split_heads((key_cache, value_cache), head_count)
    split, (query_weight, kv_weight) = lax.optimization_barrier((split, (query_weight, kv_weight)))
    key_pieces = [split[0]]
    for d in range(1, head_count):
        key_pieces.append(lax.ppermute(split[d], "head", xor_pairs("head", d)))
    for d in range(head_count):
        key_pieces.append(swap_cores(key_pieces[d]))
    pair = arrange(key_pieces)

    positions = jnp.arange(SL, dtype=jnp.int32)
    own_position = parity * SL + positions

    def with_reach(own_values, other_values):
        reach = lax.dynamic_slice_in_dim(other_values, parity * (SL - REACH), REACH)
        return jnp.concatenate([own_values, reach])

    key_position = with_reach(own_position, (1 - parity) * SL + positions)
    key_segments = with_reach(segment_ids, other_segments)
    key_flags = with_reach(image_flags, other_flags)
    visible = (segment_ids[:, None] == key_segments[None, :]) & (
        (key_position[None, :] <= own_position[:, None])
        | ((image_flags[:, None] == 1) & (key_flags[None, :] == 1))
    )
    bias_s = jnp.where(visible, 0.0, far_negative).astype(jnp.float32)
    bias_c = jnp.where(
        jnp.arange(CTX, dtype=jnp.int32)[None, :] < cache_length[0], 0.0, far_negative
    ).astype(jnp.float32)

    query_weight = transposed(query_weight)
    other_weight = swap_cores(query_weight)
    kv_columns = [kv_weight.T]
    for d in range(1, head_count):
        kv_columns.append(lax.ppermute(kv_columns[0], "head", xor_pairs("head", d)))
    for d in range(head_count):
        kv_columns.append(swap_cores(kv_columns[d]))
    gain, bias_c = lax.optimization_barrier((gain, bias_c))

    kv_grad, pieces, spans, before, first_row = (), [], [], [], 0
    flushes = flush_points(plan)
    for c, (start, count) in enumerate(plan):
        kv_grad, parts = attention(
            stash[c],
            token_block(out_grad, start, count, head_count, 16),
            pair,
            bias_c,
            token_block(bias_s, start, count, head_count, 8),
            kv_grad,
            before,
            (query_weight, other_weight) if c in flushes else None,
            head_count,
            VMEM_LIMIT if c + 1 < len(plan) else LAST_VMEM_LIMIT,
        )
        if c not in flushes:
            before = before + list(parts)
            continue
        for d, part in enumerate(parts):
            pieces.append(lax.ppermute(part, "head", xor_pairs("head", d)) if d else part)
        spans.append((first_row, start + count - first_row))
        first_row, before = start + count, []
    received = swap_cores(kv_grad[1])
    share_dtype = jnp.bfloat16 if sharers == 1 else jnp.float32
    shares = list(share_kv(kv_grad[0], received, head_count, share_dtype))
    for d in range(1, head_count):
        shares[d] = lax.ppermute(shares[d], "head", xor_pairs("head", d))
    return finish(
        gain, layer_input, residual_grad, shares, pieces, spent, kv_columns, spans
    )


def solution(mesh):
    return jax.shard_map(
        body,
        mesh=mesh,
        in_specs=(
            P("section", "head"),
            P("section", "head"),
            P("section", "head"),
            P(("section", "head"), None),
            P(("section", "head"), None),
            P("section"),
            P("section"),
            P("section"),
            P("section", "head"),
            P("section", "head"),
            P("section"),
            P(("section", "head"), None),
            P(("section", "head"), None),
        ),
        out_specs=P(("section", "head"), None),
        check_vma=False,
    )
```

time: 212 us -> 220 us (1.038)
  waiting for transfers between devices: 43.3 us -> 87.9 us
  local copies, waits for them, and re-layouts: 32.4 us -> 7.9 us
  Pallas kernels: 60.8 us -> 52.5 us
  starting transfers between devices: 72 us -> 69.5 us
    unnamed x88 -> x22, local copies, waits for them, and re-layouts: 29.2 us -> 3.01 us
    ppermute x9 -> x8, waiting for transfers between devices: 7.5 us -> 32.5 us  [the longest x3 32.5 us: body(): kv_columns.append(lax.ppermute(kv_columns[0], 'head', xor_pairs('head', d)))]
    pallas_call x3, Pallas kernels: 48.9 us -> 34 us  [attention(): pl.pallas_call(functools.partial(attention_kernel, tokens=tokens, local_h...]
    ppermute x4, waiting for transfers between devices: 22.9 us -> 33.3 us  [body(): stash[-1].append(lax.ppermute(buffer, 'section', mirror))]
    ppermute x10 -> x13, waiting for transfers between devices: 0.65 us -> 9.44 us  [swap_cores(): return lax.ppermute(value, 'section', xor_pairs('section', 1))]
    pallas_call x1 -> x4, Pallas kernels: 1.86 us -> 9.48 us  [the longest x1 8.09 us: transposed(): pl.pallas_call(transpose_kernel, out_shape=jax.ShapeDtypeStruct((columns,...]
    ppermute x9 -> x6, starting transfers between devices: 11.2 us -> 5.15 us  [body(): lax.ppermute(part, 'head', xor_pairs('head', d))]
    ppermute x3, waiting for transfers between devices: 0.35 us -> 3.05 us  [body(): shares[d] = lax.ppermute(shares[d], 'head', xor_pairs('head', d))]
  transfers between devices with their start and end apart: 35 -> 34, of which waited for: 11 -> 13; matrix products, arithmetic and copies ran while one was open for 1% -> 1% of each run, Pallas kernels for 24% -> 16%
where the time goes in v2:
time: 220 us; the launch traced here: 219 us
  waiting for transfers between devices  87.9 us (40%)
  starting transfers between devices  69.5 us (32%)
  Pallas kernels  52.5 us (24%)
  local copies, waits for them, and re-layouts  7.9 us (4%)
    ppermute x2, starting transfers between devices, body(): spent.append(lax.ppermute(group[0] if c else held_query, 'section', inward))  36.7 us
    pallas_call x3, Pallas kernels, attention(): pl.pallas_call(functools.partial(attention_kernel, tokens=tokens, local_h...  34 us
    ppermute x4, waiting for transfers between devices, body(): stash[-1].append(lax.ppermute(buffer, 'section', mirror))  33.3 us
    ppermute x3, waiting for transfers between devices, body(): kv_columns.append(lax.ppermute(kv_columns[0], 'head', xor_pairs('head', d)))  32.5 us
    ppermute x4, starting transfers between devices, body(): stash[-1].append(lax.ppermute(buffer, 'section', mirror))  10.5 us
    ppermute x6, waiting for transfers between devices, body(): lax.ppermute(part, 'head', xor_pairs('head', d))  9.58 us
    ppermute x13, waiting for transfers between devices, swap_cores(): return lax.ppermute(value, 'section', xor_pairs('section', 1))  9.44 us
    pallas_call x1, Pallas kernels, transposed(): pl.pallas_call(transpose_kernel, out_shape=jax.ShapeDtypeStruct((columns,...  8.09 us
  transfers between devices with their start and end apart: 34, of which 13 were waited for; matrix products, arithmetic and copies ran while one was open for 1% of the time, Pallas kernels for 16%

profile of v2, /device:TPU:0, one launch (start us, length us, event | category | flops | bytes accessed | tf_op | source)
XLA Modules:
  0.0 219.2 jit_solution(2216191336935478693)
XLA Ops:
  0.0 1.9 slice.8
  1.9 1.1 slice.9
  3.0 3.6 %pack.1 = (bf16[2,64,2048]{2,1,0:T(8,128)(2,1)}, bf16[2,64,2048]{2,1,0:T(8,128)(2,1)}) custom-call(bf16[256,2048]{1,0:T(8,128)(2,1)} %q_ref, bf16[256,2048]{1,0:T(8,128)(2,1)} %o_ref), custom_call_target="tpu_custom_call" | custom-call | tf_op jit(solution)/shard_map/pack/pallas_call | solution.py:345
  6.6 1.0 copy-done.2
  7.6 1.0 copy-done.3
  8.6 0.8 split.1
  9.4 8.1 %transposed.1.refs_8_.refs_7_ = bf16[2048,2048]{1,0:T(8,128)(2,1)} custom-call(bf16[2048,2048]{1,0:T(8,128)(2,1)} %in_ref), custom_call_target="tpu_custom_call" | custom-call | flops 4194304 | bytes 16777216 | tf_op jit(solution)/shard_map/transposed/pallas_call | solution.py:369
  17.5 0.5 collective-permute-start.14
  18.0 2.5 %collective-permute-start.2 = (bf16[2,320,128]{2,1,0:T(8,128)(2,1)}, bf16[2,320,128]{2,1,0:T(8,128)(2,1)S(1)}, u32[]{:S(2)}, u32[]{:S(2)}) collective-permute-start(bf16[2,320,128]{2,1,0:T(8,128)(2,1)} %get-tuple-element.64), channel_id=1, source_target_pairs={{0,1},{1,0},{2,3},{3,2},{4,5},{5,4},{6,7},{7,6},{8,9},{9,8},{10,11... | collective-permute-start | bytes 491528 | tf_op jit(solution)/shard_map/ppermute | solution.py:584
  20.5 1.5 collective-permute-start.3
  22.0 0.5 collective-permute-start.10
  23.2 0.1 dynamic_slice.10
  23.3 0.1 eq.40
  23.4 0.1 and.27
  23.5 1.5 copy.14
  25.0 6.1 %collective-permute-done.9 = s32[256]{0:T(256)S(1)} collective-permute-done((s32[256]{0:T(256)S(1)}, s32[256]{0:T(256)S(1)}, u32[]{:S(2)}, u32[]{:S(2)}) %collective-permute-start.9) | collective-permute-done | bytes 1056 | tf_op jit(solution)/shard_map/ppermute | solution.py:545
  31.1 3.8 %collective-permute-start.4 = (bf16[2,320,128]{2,1,0:T(8,128)(2,1)S(1)}, bf16[2,320,128]{2,1,0:T(8,128)(2,1)S(1)}, u32[]{:S(2)}, u32[]{:S(2)}) collective-permute-start(bf16[2,320,128]{2,1,0:T(8,128)(2,1)S(1)} %get-tuple-element.66), channel_id=1, source_target_pairs={{0,3},{1,2},{2,1},{3,0},{4,7},{5,6},{6,5},{7,4},{8,11},{9,10},{10,... | collective-permute-start | bytes 491528 | tf_op jit(solution)/shard_map/ppermute | solution.py:584
  34.9 0.1 dynamic_slice.9
  35.0 0.1 collective-permute-start
  35.1 0.1 dynamic_slice.11
  35.2 1.1 collective-permute-done
  36.2 3.6 %collective-permute-start.13 = (bf16[128,2048]{1,0:T(8,128)(2,1)S(1)}, bf16[128,2048]{1,0:T(8,128)(2,1)S(1)}, u32[]{:S(2)}, u32[]{:S(2)}) collective-permute-start(bf16[128,2048]{1,0:T(8,128)(2,1)S(1)} %bitcast.18), channel_id=1, source_target_pairs={{0,24},{4,28},{8,16},{12,20},{16,8},{20,12},{24,0},{28,4},{1,25},{... | collective-permute-start | bytes 1572872 | tf_op jit(solution)/shard_map/ppermute | solution.py:571
  39.9 0.3 collective-permute-start.12
  40.2 0.3 collective-permute-start.6
  40.4 0.2 and_select_fusion.refs_5_.refs_4_
  40.7 0.6 collective-permute-done.5.refs_4_
  41.2 0.1 collective-permute-start.7
  41.4 0.2 collective-permute-done.6.refs_5_
  41.5 0.3 collective-permute-start.8
  41.9 0.8 collective-permute-done.7.refs_6_
  42.6 3.0 %collective-permute-start.11 = (bf16[2,64,2048]{2,1,0:T(8,128)(2,1)}, bf16[2,64,2048]{2,1,0:T(8,128)(2,1)S(1)}, u32[]{:S(2)}, u32[]{:S(2)}) collective-permute-start(bf16[2,64,2048]{2,1,0:T(8,128)(2,1)} %get-tuple-element.68), channel_id=1, source_target_pairs={{0,24},{4,28},{8,16},{12,20},{16,8},{20,12},{24,0},{28,4},{1,25},{... | collective-permute-start | bytes 1572872 | tf_op jit(solution)/shard_map/ppermute | solution.py:571
  45.6 1.3 collective-permute-start.26
  46.9 0.1 arrange.1.refs_3_.refs_2_
  47.0 17.1 %collective-permute-done.12.refs_0_ = bf16[128,2048]{1,0:T(8,128)(2,1)S(1)} collective-permute-done((bf16[128,2048]{1,0:T(8,128)(2,1)}, bf16[128,2048]{1,0:T(8,128)(2,1)S(1)}, u32[]{:S(2)}, u32[]{:S(2)}) %collective-permute-start.12) | collective-permute-done | bytes 524320 | tf_op jit(solution)/shard_map/ppermute | solution.py:571
  64.2 3.6 %collective-permute-start.1 = (bf16[2,64,2048]{2,1,0:T(8,128)(2,1)}, bf16[2,64,2048]{2,1,0:T(8,128)(2,1)S(1)}, u32[]{:S(2)}, u32[]{:S(2)}) collective-permute-start(bf16[2,64,2048]{2,1,0:T(8,128)(2,1)} %get-tuple-element.54), channel_id=1, source_target_pairs={{0,24},{4,28},{8,16},{12,20},{16,8},{20,12},{24,0},{28,4},{1,25},{... | collective-permute-start | bytes 1572872 | tf_op jit(solution)/shard_map/ppermute | solution.py:571
  67.8 0.5 collective-permute-start.27
  68.3 12.7 %attention.3 = (f32[256,256]{1,0:T(8,128)S(1)}, f32[256,128]{1,0:T(8,128)S(1)}, bf16[128,2048]{1,0:T(8,128)(2,1)S(1)}) custom-call(bf16[128,2048]{1,0:T(8,128)(2,1)S(1)} %collective-permute-done.12.refs_0_, bf16[128,2048]{1,0:T(8,128)(2,1)S(1)} %collective-permute-done.13.refs_1_, bf16[4,64,2048]{2,1,0:T(8,128)(2,1)S(1)} %bitcast.13, ...), custom_call_target="tpu_custom_call" | custom-call | flops 15300820992 | bytes 3342336 | tf_op jit(solution)/shard_map/attention/pallas_call | solution.py:258
  81.0 16.2 %collective-permute-done.1.refs_0_ = bf16[2,64,2048]{2,1,0:T(8,128)(2,1)S(1)} collective-permute-done((bf16[2,64,2048]{2,1,0:T(8,128)(2,1)}, bf16[2,64,2048]{2,1,0:T(8,128)(2,1)S(1)}, u32[]{:S(2)}, u32[]{:S(2)}) %collective-permute-start.1) | collective-permute-done | bytes 524320 | tf_op jit(solution)/shard_map/ppermute | solution.py:571
  97.2 35.4 %collective-permute-start.25 = (bf16[256,2048]{1,0:T(8,128)(2,1)S(1)}, bf16[256,2048]{1,0:T(8,128)(2,1)S(1)}, u32[]{:S(2)}, u32[]{:S(2)}) collective-permute-start(bf16[256,2048]{1,0:T(8,128)(2,1)S(1)} %copy-done.7), channel_id=1, source_target_pairs={{0,8},{4,12},{24,16},{28,20},{1,9},{5,13},{25,17},{29,21},{2,10},{... | collective-permute-start | bytes 3145736 | tf_op jit(solution)/shard_map/ppermute | solution.py:573
  132.6 0.6 collective-permute-start.28
  133.2 1.5 collective-permute-start.29
  134.7 0.5 collective-permute-start.31
  135.2 11.6 %attention.4 = (f32[256,256]{1,0:T(8,128)S(1)}, f32[256,128]{1,0:T(8,128)S(1)}, bf16[48,4096]{1,0:T(8,128)(2,1)S(1)}, bf16[48,4096]{1,0:T(8,128)(2,1)}, bf16[48,...) custom-call(bf16[2,64,2048]{2,1,0:T(8,128)(2,1)S(1)} %collective-permute-done.11.refs_0_, ...), custom_call_target="tpu_custom_call" | custom-call | flops 20535312384 | bytes 2293760 | tf_op jit(solution)/shard_map/attention/pallas_call | solution.py:258
  146.8 32.5 %collective-permute-done.28.refs_19_ = bf16[256,2048]{1,0:T(8,128)(2,1)S(1)} collective-permute-done((bf16[256,2048]{1,0:T(8,128)(2,1)S(1)}, bf16[256,2048]{1,0:T(8,128)(2,1)S(1)}, u32[]{:S(2)}, u32[]{:S(2)}) %collective-permute-start.28) | collective-permute-done | bytes 1048608 | tf_op jit(solution)/shard_map/ppermute | solution.py:612
  179.3 0.5 collective-permute-start.33
  179.8 0.5 collective-permute-start.19
  180.3 0.5 collective-permute-start.20
  180.8 2.4 %collective-permute-start.21 = (bf16[48,4096]{1,0:T(8,128)(2,1)S(1)}, bf16[48,4096]{1,0:T(8,128)(2,1)S(1)}, u32[]{:S(2)}, u32[]{:S(2)}) collective-permute-start(bf16[48,4096]{1,0:T(8,128)(2,1)S(1)} %get-tuple-element.85), channel_id=1, source_target_pairs={{0,3},{1,2},{2,1},{3,0},{4,7},{5,6},{6,5},{7,4},{8,11},{9,10},{10,... | collective-permute-start | bytes 1179656 | tf_op jit(solution)/shard_map/ppermute | solution.py:636
  183.3 1.0 copy-done.6
  184.3 9.8 %attention.5 = (f32[256,256]{1,0:T(8,128)S(1)}, f32[256,128]{1,0:T(8,128)S(1)}, bf16[16,4096]{1,0:T(8,128)(2,1)S(1)}, bf16[16,4096]{1,0:T(8,128)(2,1)S(1)}, bf16...) custom-call(bf16[2,64,2048]{2,1,0:T(8,128)(2,1)S(1)} %copy-done.6, bf16[4,64,2048]{2,1,0:T(8,128)(2,1)S(1)} %bitcast.15, ...), custom_call_target="tpu_custom_call" | custom-call | flops 11945377792 | bytes 2293760 | tf_op jit(solution)/shard_map/attention/pallas_call | solution.py:258
  194.1 0.1 collective-permute-start.15
  194.2 0.6 collective-permute-start.22
  194.8 0.7 collective-permute-done.15.recv_ref
  195.5 0.5 collective-permute-start.23
  196.1 6.2 %collective-permute-done.22.refs_12_ = bf16[16,4096]{1,0:T(8,128)(2,1)S(1)} collective-permute-done((bf16[16,4096]{1,0:T(8,128)(2,1)S(1)}, bf16[16,4096]{1,0:T(8,128)(2,1)S(1)}, u32[]{:S(2)}, u32[]{:S(2)}) %collective-permute-start.22) | collective-permute-done | bytes 131104 | tf_op jit(solution)/shard_map/ppermute | solution.py:636
  202.3 0.5 collective-permute-start.24
  202.8 0.4 share.1
  203.3 1.6 collective-permute-start.16
  204.8 3.3 %collective-permute-done.24.refs_14_ = bf16[16,4096]{1,0:T(8,128)(2,1)S(1)} collective-permute-done((bf16[16,4096]{1,0:T(8,128)(2,1)S(1)}, bf16[16,4096]{1,0:T(8,128)(2,1)S(1)}, u32[]{:S(2)}, u32[]{:S(2)}) %collective-permute-start.24) | collective-permute-done | bytes 131104 | tf_op jit(solution)/shard_map/ppermute | solution.py:636
  208.2 0.6 collective-permute-start.17
  208.7 1.8 collective-permute-start.18
  210.5 1.6 collective-permute-done.17.refs_5_
  212.1 1.5 collective-permute-done.18.refs_6_
  213.6 5.4 %finish.1 = bf16[64,4096]{1,0:T(8,128)(2,1)} custom-call(bf16[1,4096]{1,0:T(2,128)(2,1)S(1)} %broadcast_select_fusion.refs_0_, bf16[64,4096]{1,0:T(8,128)(2,1)S(1)} %copy-done, bf16[64,4096]{1,0:T(8,128)(2,1)S(1)} %copy-done.1, bf16[64,256]{1,0:T(8,128)(2,1)S(1)} %get-tuple-element.78.refs_3_, bf16[64,256]{1,0:T(8,128)(2,1)S(1)} %collective-permute-done.16.refs_4_, ...), custom_call_target="tpu_custom_call" | custom-call | flops 1073741824 | bytes 8388608 | tf_op jit(solution)/shard_map/finish/pallas_call | solution.py:492
  (55 shorter events, 0.2 us)
Async XLA Ops:
  6.6 1.0 copy-start.2
  7.6 1.0 copy-start.3
  9.4 12.6 %copy-start.9 = (s32[256]{0:T(256)S(1)}, s32[256]{0:T(256)}, u32[]{:S(2)}) copy-start(s32[256]{0:T(256)} %param.18) | copy-start | bytes 3076
  9.4 12.6 %copy-start.10 = (s32[256]{0:T(256)S(1)}, s32[256]{0:T(256)}, u32[]{:S(2)}) copy-start(s32[256]{0:T(256)} %param.19) | copy-start | bytes 3076
  9.4 14.0 %copy-start.8 = (bf16[2048]{0:T(1024)(128)(2,1)S(1)}, bf16[2048]{0:T(1024)(128)(2,1)}, u32[]{:S(2)}) copy-start(bf16[2048]{0:T(1024)(128)(2,1)} %param.23) | copy-start | bytes 12292
  9.4 58.9 %copy-start.4 = (bf16[256,2048]{1,0:T(8,128)(2,1)S(1)}, bf16[256,2048]{1,0:T(8,128)(2,1)}, u32[]{:S(2)}) copy-start(bf16[256,2048]{1,0:T(8,128)(2,1)} %param.13) | copy-start | bytes 3145732
  17.5 117.2 %collective-permute-start.14 = (bf16[2048,2048]{1,0:T(8,128)(2,1)}, bf16[2048,2048]{1,0:T(8,128)(2,1)}, u32[]{:S(2)}, u32[]{:S(2)}) collective-permute-start(bf16[2048,2048]{1,0:T(8,128)(2,1)} %transposed.1.refs_8_.refs_7_), channel_id=1, source_target_pairs={{0,4},{4,0},{8,12},{12,8},{16,20},{20,16},{24,28},{28,24},{1,5},{5... | collective-permute-start | bytes 25165832 | tf_op jit(solution)/shard_map/ppermute | solution.py:545
  18.0 21.9 %collective-permute-start.2 = (bf16[2,320,128]{2,1,0:T(8,128)(2,1)}, bf16[2,320,128]{2,1,0:T(8,128)(2,1)S(1)}, u32[]{:S(2)}, u32[]{:S(2)}) collective-permute-start(bf16[2,320,128]{2,1,0:T(8,128)(2,1)} %get-tuple-element.64), channel_id=1, source_target_pairs={{0,1},{1,0},{2,3},{3,2},{4,5},{5,4},{6,7},{7,6},{8,9},{9,8},{10,11... | collective-permute-start | bytes 491528 | tf_op jit(solution)/shard_map/ppermute | solution.py:584
  20.5 19.4 %collective-permute-start.3 = (bf16[2,320,128]{2,1,0:T(8,128)(2,1)}, bf16[2,320,128]{2,1,0:T(8,128)(2,1)S(1)}, u32[]{:S(2)}, u32[]{:S(2)}) collective-permute-start(bf16[2,320,128]{2,1,0:T(8,128)(2,1)} %get-tuple-element.65), channel_id=1, source_target_pairs={{0,2},{1,3},{2,0},{3,1},{4,6},{5,7},{6,4},{7,5},{8,10},{9,11},{10,... | collective-permute-start | bytes 491528 | tf_op jit(solution)/shard_map/ppermute | solution.py:584
  22.0 9.1 %collective-permute-start.9 = (s32[256]{0:T(256)S(1)}, s32[256]{0:T(256)S(1)}, u32[]{:S(2)}, u32[]{:S(2)}) collective-permute-start(s32[256]{0:T(256)S(1)} %copy-done.9), channel_id=1, source_target_pairs={{0,4},{4,0},{8,12},{12,8},{16,20},{20,16},{24,28},{28,24},{1,5},{5... | collective-permute-start | bytes 3080 | tf_op jit(solution)/shard_map/ppermute | solution.py:545
  22.0 13.0 %collective-permute-start.10 = (s32[256]{0:T(256)S(1)}, s32[256]{0:T(256)S(1)}, u32[]{:S(2)}, u32[]{:S(2)}) collective-permute-start(s32[256]{0:T(256)S(1)} %copy-done.10), channel_id=1, source_target_pairs={{0,4},{4,0},{8,12},{12,8},{16,20},{20,16},{24,28},{28,24},{1,5},{5... | collective-permute-start | bytes 3080 | tf_op jit(solution)/shard_map/ppermute | solution.py:545
  31.1 9.0 %collective-permute-start.4 = (bf16[2,320,128]{2,1,0:T(8,128)(2,1)S(1)}, bf16[2,320,128]{2,1,0:T(8,128)(2,1)S(1)}, u32[]{:S(2)}, u32[]{:S(2)}) collective-permute-start(bf16[2,320,128]{2,1,0:T(8,128)(2,1)S(1)} %get-tuple-element.66), channel_id=1, source_target_pairs={{0,3},{1,2},{2,1},{3,0},{4,7},{5,6},{6,5},{7,4},{8,11},{9,10},{10,... | collective-permute-start | bytes 491528 | tf_op jit(solution)/shard_map/ppermute | solution.py:584
  35.0 1.2 collective-permute-start
  36.2 31.5 %collective-permute-start.13 = (bf16[128,2048]{1,0:T(8,128)(2,1)S(1)}, bf16[128,2048]{1,0:T(8,128)(2,1)S(1)}, u32[]{:S(2)}, u32[]{:S(2)}) collective-permute-start(bf16[128,2048]{1,0:T(8,128)(2,1)S(1)} %bitcast.18), channel_id=1, source_target_pairs={{0,24},{4,28},{8,16},{12,20},{16,8},{20,12},{24,0},{28,4},{1,25},{... | collective-permute-start | bytes 1572872 | tf_op jit(solution)/shard_map/ppermute | solution.py:571
  39.9 1.4 collective-permute-start.5
  39.9 24.3 %collective-permute-start.12 = (bf16[128,2048]{1,0:T(8,128)(2,1)}, bf16[128,2048]{1,0:T(8,128)(2,1)S(1)}, u32[]{:S(2)}, u32[]{:S(2)}) collective-permute-start(bf16[128,2048]{1,0:T(8,128)(2,1)} %bitcast.19), channel_id=1, source_target_pairs={{0,24},{4,28},{8,16},{12,20},{16,8},{20,12},{24,0},{28,4},{1,25},{... | collective-permute-start | bytes 1572872 | tf_op jit(solution)/shard_map/ppermute | solution.py:571
  40.2 1.4 collective-permute-start.6
  41.2 1.4 collective-permute-start.7
  41.5 4.1 %collective-permute-start.8 = (bf16[2,320,128]{2,1,0:T(8,128)(2,1)S(1)}, bf16[2,320,128]{2,1,0:T(8,128)(2,1)S(1)}, u32[]{:S(2)}, u32[]{:S(2)}) collective-permute-start(bf16[2,320,128]{2,1,0:T(8,128)(2,1)S(1)} %collective-permute-done.4.refs_3_), channel_id=1, source_target_pairs={{0,4},{4,0},{8,12},{12,8},{16,20},{20,16},{24,28},{28,24},{1,5},{5... | collective-permute-start | bytes 491528 | tf_op jit(solution)/shard_map/ppermute | solution.py:545
  42.6 90.0 %collective-permute-start.11 = (bf16[2,64,2048]{2,1,0:T(8,128)(2,1)}, bf16[2,64,2048]{2,1,0:T(8,128)(2,1)S(1)}, u32[]{:S(2)}, u32[]{:S(2)}) collective-permute-start(bf16[2,64,2048]{2,1,0:T(8,128)(2,1)} %get-tuple-element.68), channel_id=1, source_target_pairs={{0,24},{4,28},{8,16},{12,20},{16,8},{20,12},{24,0},{28,4},{1,25},{... | collective-permute-start | bytes 1572872 | tf_op jit(solution)/shard_map/ppermute | solution.py:571
  45.6 87.6 %collective-permute-start.26 = (bf16[2,64,2048]{2,1,0:T(8,128)(2,1)}, bf16[2,64,2048]{2,1,0:T(8,128)(2,1)S(1)}, u32[]{:S(2)}, u32[]{:S(2)}) collective-permute-start(bf16[2,64,2048]{2,1,0:T(8,128)(2,1)} %get-tuple-element.68), channel_id=1, source_target_pairs={{0,8},{4,12},{24,16},{28,20},{1,9},{5,13},{25,17},{29,21},{2,10},{... | collective-permute-start | bytes 1572872 | tf_op jit(solution)/shard_map/ppermute | solution.py:573
  64.2 33.0 %collective-permute-start.1 = (bf16[2,64,2048]{2,1,0:T(8,128)(2,1)}, bf16[2,64,2048]{2,1,0:T(8,128)(2,1)S(1)}, u32[]{:S(2)}, u32[]{:S(2)}) collective-permute-start(bf16[2,64,2048]{2,1,0:T(8,128)(2,1)} %get-tuple-element.54), channel_id=1, source_target_pairs={{0,24},{4,28},{8,16},{12,20},{16,8},{20,12},{24,0},{28,4},{1,25},{... | collective-permute-start | bytes 1572872 | tf_op jit(solution)/shard_map/ppermute | solution.py:571
  67.8 66.9 %collective-permute-start.27 = (bf16[256,2048]{1,0:T(8,128)(2,1)S(1)}, bf16[256,2048]{1,0:T(8,128)(2,1)S(1)}, u32[]{:S(2)}, u32[]{:S(2)}) collective-permute-start(bf16[256,2048]{1,0:T(8,128)(2,1)S(1)} %bitcast.8), channel_id=1, source_target_pairs={{0,1},{1,0},{2,3},{3,2},{4,5},{5,4},{6,7},{7,6},{8,9},{9,8},{10,11... | collective-permute-start | bytes 3145736 | tf_op jit(solution)/shard_map/ppermute | solution.py:612
  68.3 28.9 %copy-start.7 = (bf16[256,2048]{1,0:T(8,128)(2,1)S(1)}, bf16[256,2048]{1,0:T(8,128)(2,1)}, u32[]{:S(2)}) copy-start(bf16[256,2048]{1,0:T(8,128)(2,1)} %q_ref) | copy-start | bytes 3145732
  97.2 49.6 %copy-start.5 = (bf16[2,64,2048]{2,1,0:T(8,128)(2,1)}, bf16[2,64,2048]{2,1,0:T(8,128)(2,1)S(1)}, u32[]{:S(2)}) copy-start(bf16[2,64,2048]{2,1,0:T(8,128)(2,1)S(1)} %collective-permute-done.1.refs_0_) | copy-start | bytes 1572868
  97.2 82.6 %collective-permute-start.25 = (bf16[256,2048]{1,0:T(8,128)(2,1)S(1)}, bf16[256,2048]{1,0:T(8,128)(2,1)S(1)}, u32[]{:S(2)}, u32[]{:S(2)}) collective-permute-start(bf16[256,2048]{1,0:T(8,128)(2,1)S(1)} %copy-done.7), channel_id=1, source_target_pairs={{0,8},{4,12},{24,16},{28,20},{1,9},{5,13},{25,17},{29,21},{2,10},{... | collective-permute-start | bytes 3145736 | tf_op jit(solution)/shard_map/ppermute | solution.py:573
  132.6 46.6 %collective-permute-start.28 = (bf16[256,2048]{1,0:T(8,128)(2,1)S(1)}, bf16[256,2048]{1,0:T(8,128)(2,1)S(1)}, u32[]{:S(2)}, u32[]{:S(2)}) collective-permute-start(bf16[256,2048]{1,0:T(8,128)(2,1)S(1)} %bitcast.9), channel_id=1, source_target_pairs={{0,2},{1,3},{2,0},{3,1},{4,6},{5,7},{6,4},{7,5},{8,10},{9,11},{10,... | collective-permute-start | bytes 3145736 | tf_op jit(solution)/shard_map/ppermute | solution.py:612
  133.2 46.1 %collective-permute-start.29 = (bf16[256,2048]{1,0:T(8,128)(2,1)S(1)}, bf16[256,2048]{1,0:T(8,128)(2,1)S(1)}, u32[]{:S(2)}, u32[]{:S(2)}) collective-permute-start(bf16[256,2048]{1,0:T(8,128)(2,1)S(1)} %bitcast.10), channel_id=1, source_target_pairs={{0,3},{1,2},{2,1},{3,0},{4,7},{5,6},{6,5},{7,4},{8,11},{9,10},{10,... | collective-permute-start | bytes 3145736 | tf_op jit(solution)/shard_map/ppermute | solution.py:612
  134.7 45.6 %collective-permute-start.30 = (bf16[256,2048]{1,0:T(8,128)(2,1)S(1)}, bf16[256,2048]{1,0:T(8,128)(2,1)S(1)}, u32[]{:S(2)}, u32[]{:S(2)}) collective-permute-start(bf16[256,2048]{1,0:T(8,128)(2,1)S(1)} %bitcast.11), channel_id=1, source_target_pairs={{0,4},{4,0},{8,12},{12,8},{16,20},{20,16},{24,28},{28,24},{1,5},{5... | collective-permute-start | bytes 3145736 | tf_op jit(solution)/shard_map/ppermute | solution.py:545
  134.7 46.1 %collective-permute-start.31 = (bf16[256,2048]{1,0:T(8,128)(2,1)S(1)}, bf16[256,2048]{1,0:T(8,128)(2,1)S(1)}, u32[]{:S(2)}, u32[]{:S(2)}) collective-permute-start(bf16[256,2048]{1,0:T(8,128)(2,1)S(1)} %collective-permute-done.27.refs_18_), channel_id=1, source_target_pairs={{0,4},{4,0},{8,12},{12,8},{16,20},{20,16},{24,28},{28,24},{1,5},{5... | collective-permute-start | bytes 3145736 | tf_op jit(solution)/shard_map/ppermute | solution.py:545
  179.3 14.9 %collective-permute-start.32 = (bf16[256,2048]{1,0:T(8,128)(2,1)S(1)}, bf16[256,2048]{1,0:T(8,128)(2,1)S(1)}, u32[]{:S(2)}, u32[]{:S(2)}) collective-permute-start(bf16[256,2048]{1,0:T(8,128)(2,1)S(1)} %collective-permute-done.28.refs_19_), channel_id=1, source_target_pairs={{0,4},{4,0},{8,12},{12,8},{16,20},{20,16},{24,28},{28,24},{1,5},{5... | collective-permute-start | bytes 3145736 | tf_op jit(solution)/shard_map/ppermute | solution.py:545
  179.3 14.9 %collective-permute-start.33 = (bf16[256,2048]{1,0:T(8,128)(2,1)S(1)}, bf16[256,2048]{1,0:T(8,128)(2,1)S(1)}, u32[]{:S(2)}, u32[]{:S(2)}) collective-permute-start(bf16[256,2048]{1,0:T(8,128)(2,1)S(1)} %collective-permute-done.29.refs_20_), channel_id=1, source_target_pairs={{0,4},{4,0},{8,12},{12,8},{16,20},{20,16},{24,28},{28,24},{1,5},{5... | collective-permute-start | bytes 3145736 | tf_op jit(solution)/shard_map/ppermute | solution.py:545
  179.8 33.8 %collective-permute-start.19 = (bf16[48,4096]{1,0:T(8,128)(2,1)}, bf16[48,4096]{1,0:T(8,128)(2,1)S(1)}, u32[]{:S(2)}, u32[]{:S(2)}) collective-permute-start(bf16[48,4096]{1,0:T(8,128)(2,1)} %get-tuple-element.83), channel_id=1, source_target_pairs={{0,1},{1,0},{2,3},{3,2},{4,5},{5,4},{6,7},{7,6},{8,9},{9,8},{10,11... | collective-permute-start | bytes 1179656 | tf_op jit(solution)/shard_map/ppermute | solution.py:636
  180.3 33.2 %collective-permute-start.20 = (bf16[48,4096]{1,0:T(8,128)(2,1)}, bf16[48,4096]{1,0:T(8,128)(2,1)S(1)}, u32[]{:S(2)}, u32[]{:S(2)}) collective-permute-start(bf16[48,4096]{1,0:T(8,128)(2,1)} %get-tuple-element.84), channel_id=1, source_target_pairs={{0,2},{1,3},{2,0},{3,1},{4,6},{5,7},{6,4},{7,5},{8,10},{9,11},{10,... | collective-permute-start | bytes 1179656 | tf_op jit(solution)/shard_map/ppermute | solution.py:636
  180.8 32.7 %collective-permute-start.21 = (bf16[48,4096]{1,0:T(8,128)(2,1)S(1)}, bf16[48,4096]{1,0:T(8,128)(2,1)S(1)}, u32[]{:S(2)}, u32[]{:S(2)}) collective-permute-start(bf16[48,4096]{1,0:T(8,128)(2,1)S(1)} %get-tuple-element.85), channel_id=1, source_target_pairs={{0,3},{1,2},{2,1},{3,0},{4,7},{5,6},{6,5},{7,4},{8,11},{9,10},{10,... | collective-permute-start | bytes 1179656 | tf_op jit(solution)/shard_map/ppermute | solution.py:636
  183.3 1.0 copy-start.6
  184.3 29.3 %copy-start = (bf16[64,4096]{1,0:T(8,128)(2,1)S(1)}, bf16[64,4096]{1,0:T(8,128)(2,1)}, u32[]{:S(2)}) copy-start(bf16[64,4096]{1,0:T(8,128)(2,1)} %refs_1_.2) | copy-start | bytes 1572868
  184.3 29.3 %copy-start.1 = (bf16[64,4096]{1,0:T(8,128)(2,1)S(1)}, bf16[64,4096]{1,0:T(8,128)(2,1)}, u32[]{:S(2)}) copy-start(bf16[64,4096]{1,0:T(8,128)(2,1)} %refs_2_.1) | copy-start | bytes 1572868
  194.1 1.4 collective-permute-start.15
  194.2 8.1 %collective-permute-start.22 = (bf16[16,4096]{1,0:T(8,128)(2,1)S(1)}, bf16[16,4096]{1,0:T(8,128)(2,1)S(1)}, u32[]{:S(2)}, u32[]{:S(2)}) collective-permute-start(bf16[16,4096]{1,0:T(8,128)(2,1)S(1)} %get-tuple-element.87), channel_id=1, source_target_pairs={{0,1},{1,0},{2,3},{3,2},{4,5},{5,4},{6,7},{7,6},{8,9},{9,8},{10,11... | collective-permute-start | bytes 393224 | tf_op jit(solution)/shard_map/ppermute | solution.py:636
  195.5 7.7 %collective-permute-start.23 = (bf16[16,4096]{1,0:T(8,128)(2,1)S(1)}, bf16[16,4096]{1,0:T(8,128)(2,1)S(1)}, u32[]{:S(2)}, u32[]{:S(2)}) collective-permute-start(bf16[16,4096]{1,0:T(8,128)(2,1)S(1)} %get-tuple-element.88), channel_id=1, source_target_pairs={{0,2},{1,3},{2,0},{3,1},{4,6},{5,7},{6,4},{7,5},{8,10},{9,11},{10,... | collective-permute-start | bytes 393224 | tf_op jit(solution)/shard_map/ppermute | solution.py:636
  202.3 5.9 %collective-permute-start.24 = (bf16[16,4096]{1,0:T(8,128)(2,1)S(1)}, bf16[16,4096]{1,0:T(8,128)(2,1)S(1)}, u32[]{:S(2)}, u32[]{:S(2)}) collective-permute-start(bf16[16,4096]{1,0:T(8,128)(2,1)S(1)} %get-tuple-element.89), channel_id=1, source_target_pairs={{0,3},{1,2},{2,1},{3,0},{4,7},{5,6},{6,5},{7,4},{8,11},{9,10},{10,... | collective-permute-start | bytes 393224 | tf_op jit(solution)/shard_map/ppermute | solution.py:636
  203.3 5.4 %collective-permute-start.16 = (bf16[64,256]{1,0:T(8,128)(2,1)S(1)}, bf16[64,256]{1,0:T(8,128)(2,1)S(1)}, u32[]{:S(2)}, u32[]{:S(2)}) collective-permute-start(bf16[64,256]{1,0:T(8,128)(2,1)S(1)} %get-tuple-element.79), channel_id=1, source_target_pairs={{0,1},{1,0},{2,3},{3,2},{4,5},{5,4},{6,7},{7,6},{8,9},{9,8},{10,11... | collective-permute-start | bytes 98312 | tf_op jit(solution)/shard_map/ppermute | solution.py:643
  208.2 3.9 %collective-permute-start.17 = (bf16[64,256]{1,0:T(8,128)(2,1)S(1)}, bf16[64,256]{1,0:T(8,128)(2,1)S(1)}, u32[]{:S(2)}, u32[]{:S(2)}) collective-permute-start(bf16[64,256]{1,0:T(8,128)(2,1)S(1)} %get-tuple-element.80), channel_id=1, source_target_pairs={{0,2},{1,3},{2,0},{3,1},{4,6},{5,7},{6,4},{7,5},{8,10},{9,11},{10,... | collective-permute-start | bytes 98312 | tf_op jit(solution)/shard_map/ppermute | solution.py:643
  208.7 4.8 %collective-permute-start.18 = (bf16[64,256]{1,0:T(8,128)(2,1)S(1)}, bf16[64,256]{1,0:T(8,128)(2,1)S(1)}, u32[]{:S(2)}, u32[]{:S(2)}) collective-permute-start(bf16[64,256]{1,0:T(8,128)(2,1)S(1)} %get-tuple-element.81), channel_id=1, source_target_pairs={{0,3},{1,2},{2,1},{3,0},{4,7},{5,6},{6,5},{7,4},{8,11},{9,10},{10,... | collective-permute-start | bytes 98312 | tf_op jit(solution)/shard_map/ppermute | solution.py:643

commit v3 on v2

--- a/solution.py
+++ b/solution.py
@@ -21,7 +21,7 @@
 log2_factor = factor * math.log2(math.e)
 
 CHUNK_EIGHTHS = (4, 2, 2)
-ROW_BLOCK = 512
+ROW_BLOCK = 1024
 KEY_BLOCK = 512
 FEATURE_TILE = 1024
 VMEM_LIMIT = 46 * 2**20
@@ -424,7 +424,8 @@
     weight_sources, refs = refs[:2 * head_count], refs[2 * head_count:]
     out_ref, refs = refs[0], refs[1:]
     locals_, refs = refs[:inputs], refs[inputs:]
-    gathered, total_ref, input_sems = refs
+    gathered, total_ref, fetched, input_sems, fetch_sems = refs
+    distant = range(2, head_count + 1)
     parity, head = lax.axis_index("section") % 2, lax.axis_index("head")
     sharers = head_count // KVH
     width, half = weight_sources[0].shape
@@ -433,7 +434,15 @@
     def input_copy(index):
         return pltpu.make_async_copy(sources[index], locals_[index], input_sems.at[index])
 
-    for index in range(inputs):
+    def fetch(index):
+        slot = index - distant.start
+        return pltpu.make_async_copy(weight_sources[index], fetched.at[slot], fetch_sems.at[slot])
+
+    for index in range(3, 3 + head_count):
+        input_copy(index).start()
+    for index in distant:
+        fetch(index).start()
+    for index in [*range(3), *range(3 + head_count, inputs)]:
         input_copy(index).start()
     gain_ref, x_ref, res_ref = locals_[:3]
     kv_pieces, pieces = locals_[3:3 + head_count], locals_[3 + head_count:]
@@ -457,10 +466,17 @@
     for side in range(2):
         place = parity if side == 0 else 1 - parity
         lanes = pl.ds(pl.multiple_of(place * half, half), half)
+        order = [d for d in range(head_count) if side * head_count + d not in distant]
+        order += [d for d in range(head_count) if side * head_count + d in distant]
         terms = []
-        for d in range(head_count):
+        for d in order:
+            index = side * head_count + d
             left = gathered[head ^ d].astype(jnp.bfloat16)
-            terms.append(dot(left, weight_sources[side * head_count + d][...], NN))
+            if index in distant:
+                fetch(index).wait()
+                terms.append(dot(left, fetched[index - distant.start], NN))
+            else:
+                terms.append(dot(left, weight_sources[index][...], NN))
         total_ref[:, lanes] = fold(jnp.add, terms)
     for index in [*range(3), *range(3 + head_count, inputs)]:
         input_copy(index).wait()
@@ -496,13 +512,18 @@
         out_shape=jax.ShapeDtypeStruct(x.shape, jnp.bfloat16),
         in_specs=[pl.BlockSpec(memory_space=space) for space in spaces]
         + [pl.BlockSpec(memory_space=pltpu.HBM) for _ in spent]
-        + [pl.BlockSpec(memory_space=pltpu.VMEM) for _ in weights],
+        + [
+            pl.BlockSpec(memory_space=pltpu.HBM if 2 <= index <= head_count else pltpu.VMEM)
+            for index in range(len(weights))
+        ],
         out_specs=pl.BlockSpec(memory_space=pltpu.VMEM),
         scratch_shapes=[pltpu.VMEM(array.shape, array.dtype) for array in local]
         + [
             pltpu.VMEM((head_count, rows, width), jnp.float32),
             pltpu.VMEM((rows, 2 * half), jnp.float32),
+            pltpu.VMEM((head_count - 1, width, half), jnp.bfloat16),
             pltpu.SemaphoreType.DMA((len(local),)),
+            pltpu.SemaphoreType.DMA((head_count - 1,)),
         ],
         compiler_params=pltpu.CompilerParams(vmem_limit_bytes=24*2**20),
         cost_estimate=pl.CostEstimate(

time: 220 us -> 220 us (level)
  transfers between devices with their start and end apart: 34 -> 34, of which waited for: 13 -> 13; matrix products, arithmetic and copies ran while one was open for 1% -> 1% of each run, Pallas kernels for 16% -> 15%
where the time goes in v3:
time: 220 us
  waiting for transfers between devices  89.1 us (40%)
  starting transfers between devices  69.2 us (31%)
  Pallas kernels  52.3 us (24%)
  local copies, waits for them, and re-layouts  7.9 us (4%)
    ppermute x2, starting transfers between devices, body(): spent.append(lax.ppermute(group[0] if c else held_query, 'section', inward))  36.7 us
    ppermute x4, waiting for transfers between devices, body(): stash[-1].append(lax.ppermute(buffer, 'section', mirror))  33.8 us
    pallas_call x3, Pallas kernels, attention(): pl.pallas_call(functools.partial(attention_kernel, tokens=tokens, local_h...  33.3 us
    ppermute x3, waiting for transfers between devices, body(): kv_columns.append(lax.ppermute(kv_columns[0], 'head', xor_pairs('head', d)))  32.5 us
    ppermute x4, starting transfers between devices, body(): stash[-1].append(lax.ppermute(buffer, 'section', mirror))  10.5 us
    ppermute x6, waiting for transfers between devices, body(): lax.ppermute(part, 'head', xor_pairs('head', d))  10.1 us
    ppermute x13, waiting for transfers between devices, swap_cores(): return lax.ppermute(value, 'section', xor_pairs('section', 1))  9.45 us
    pallas_call x1, Pallas kernels, transposed(): pl.pallas_call(transpose_kernel, out_shape=jax.ShapeDtypeStruct((columns,...  8.09 us
  transfers between devices with their start and end apart: 34, of which 13 were waited for; matrix products, arithmetic and copies ran while one was open for 1% of the time, Pallas kernels for 15%

profile of v3, /device:TPU:0, one launch (start us, length us, event | category | flops | bytes accessed | tf_op | source)
XLA Modules:
  0.0 219.9 jit_solution(8460351736906915493)
XLA Ops:
  0.0 1.9 slice.8
  1.9 1.1 slice.9
  3.0 3.6 %pack.1 = (bf16[2,64,2048]{2,1,0:T(8,128)(2,1)}, bf16[2,64,2048]{2,1,0:T(8,128)(2,1)}) custom-call(bf16[256,2048]{1,0:T(8,128)(2,1)} %q_ref, bf16[256,2048]{1,0:T(8,128)(2,1)} %o_ref), custom_call_target="tpu_custom_call" | custom-call | tf_op jit(solution)/shard_map/pack/pallas_call | solution.py:345
  6.6 1.0 copy-done.2
  7.6 1.0 copy-done.3
  8.6 0.8 split.1
  9.4 8.1 %transposed.1.refs_8_.refs_7_ = bf16[2048,2048]{1,0:T(8,128)(2,1)} custom-call(bf16[2048,2048]{1,0:T(8,128)(2,1)} %in_ref), custom_call_target="tpu_custom_call" | custom-call | flops 4194304 | bytes 16777216 | tf_op jit(solution)/shard_map/transposed/pallas_call | solution.py:369
  17.5 0.5 collective-permute-start.14
  18.0 2.5 %collective-permute-start.2 = (bf16[2,320,128]{2,1,0:T(8,128)(2,1)}, bf16[2,320,128]{2,1,0:T(8,128)(2,1)S(1)}, u32[]{:S(2)}, u32[]{:S(2)}) collective-permute-start(bf16[2,320,128]{2,1,0:T(8,128)(2,1)} %get-tuple-element.64), channel_id=1, source_target_pairs={{0,1},{1,0},{2,3},{3,2},{4,5},{5,4},{6,7},{7,6},{8,9},{9,8},{10,11... | collective-permute-start | bytes 491528 | tf_op jit(solution)/shard_map/ppermute | solution.py:605
  20.5 1.5 collective-permute-start.3
  22.0 0.5 collective-permute-start.10
  23.2 0.1 dynamic_slice.10
  23.3 0.1 eq.40
  23.4 0.1 and.27
  23.5 1.5 copy.14
  25.0 6.1 %collective-permute-done.9 = s32[256]{0:T(256)S(1)} collective-permute-done((s32[256]{0:T(256)S(1)}, s32[256]{0:T(256)S(1)}, u32[]{:S(2)}, u32[]{:S(2)}) %collective-permute-start.9) | collective-permute-done | bytes 1056 | tf_op jit(solution)/shard_map/ppermute | solution.py:566
  31.1 3.8 %collective-permute-start.4 = (bf16[2,320,128]{2,1,0:T(8,128)(2,1)S(1)}, bf16[2,320,128]{2,1,0:T(8,128)(2,1)S(1)}, u32[]{:S(2)}, u32[]{:S(2)}) collective-permute-start(bf16[2,320,128]{2,1,0:T(8,128)(2,1)S(1)} %get-tuple-element.66), channel_id=1, source_target_pairs={{0,3},{1,2},{2,1},{3,0},{4,7},{5,6},{6,5},{7,4},{8,11},{9,10},{10,... | collective-permute-start | bytes 491528 | tf_op jit(solution)/shard_map/ppermute | solution.py:605
  34.9 0.1 dynamic_slice.9
  35.0 0.1 collective-permute-start
  35.1 0.1 dynamic_slice.11
  35.2 1.1 collective-permute-done
  36.2 3.6 %collective-permute-start.13 = (bf16[128,2048]{1,0:T(8,128)(2,1)S(1)}, bf16[128,2048]{1,0:T(8,128)(2,1)S(1)}, u32[]{:S(2)}, u32[]{:S(2)}) collective-permute-start(bf16[128,2048]{1,0:T(8,128)(2,1)S(1)} %bitcast.18), channel_id=1, source_target_pairs={{0,24},{4,28},{8,16},{12,20},{16,8},{20,12},{24,0},{28,4},{1,25},{... | collective-permute-start | bytes 1572872 | tf_op jit(solution)/shard_map/ppermute | solution.py:592
  39.9 0.3 collective-permute-start.12
  40.2 0.3 collective-permute-start.6
  40.4 0.2 and_select_fusion.refs_5_.refs_4_
  40.7 0.6 collective-permute-done.5.refs_4_
  41.2 0.1 collective-permute-start.7
  41.4 0.2 collective-permute-done.6.refs_5_
  41.5 0.3 collective-permute-start.8
  41.9 0.8 collective-permute-done.7.refs_6_
  42.6 3.0 %collective-permute-start.11 = (bf16[2,64,2048]{2,1,0:T(8,128)(2,1)}, bf16[2,64,2048]{2,1,0:T(8,128)(2,1)S(1)}, u32[]{:S(2)}, u32[]{:S(2)}) collective-permute-start(bf16[2,64,2048]{2,1,0:T(8,128)(2,1)} %get-tuple-element.68), channel_id=1, source_target_pairs={{0,24},{4,28},{8,16},{12,20},{16,8},{20,12},{24,0},{28,4},{1,25},{... | collective-permute-start | bytes 1572872 | tf_op jit(solution)/shard_map/ppermute | solution.py:592
  45.6 1.3 collective-permute-start.26
  46.9 0.1 arrange.1.refs_3_.refs_2_
  47.0 17.1 %collective-permute-done.12.refs_0_ = bf16[128,2048]{1,0:T(8,128)(2,1)S(1)} collective-permute-done((bf16[128,2048]{1,0:T(8,128)(2,1)}, bf16[128,2048]{1,0:T(8,128)(2,1)S(1)}, u32[]{:S(2)}, u32[]{:S(2)}) %collective-permute-start.12) | collective-permute-done | bytes 524320 | tf_op jit(solution)/shard_map/ppermute | solution.py:592
  64.2 3.6 %collective-permute-start.1 = (bf16[2,64,2048]{2,1,0:T(8,128)(2,1)}, bf16[2,64,2048]{2,1,0:T(8,128)(2,1)S(1)}, u32[]{:S(2)}, u32[]{:S(2)}) collective-permute-start(bf16[2,64,2048]{2,1,0:T(8,128)(2,1)} %get-tuple-element.54), channel_id=1, source_target_pairs={{0,24},{4,28},{8,16},{12,20},{16,8},{20,12},{24,0},{28,4},{1,25},{... | collective-permute-start | bytes 1572872 | tf_op jit(solution)/shard_map/ppermute | solution.py:592
  67.8 0.5 collective-permute-start.27
  68.3 12.2 %attention.3 = (f32[256,256]{1,0:T(8,128)S(1)}, f32[256,128]{1,0:T(8,128)S(1)}, bf16[128,2048]{1,0:T(8,128)(2,1)S(1)}) custom-call(bf16[128,2048]{1,0:T(8,128)(2,1)S(1)} %collective-permute-done.12.refs_0_, bf16[128,2048]{1,0:T(8,128)(2,1)S(1)} %collective-permute-done.13.refs_1_, bf16[4,64,2048]{2,1,0:T(8,128)(2,1)S(1)} %bitcast.13, ...), custom_call_target="tpu_custom_call" | custom-call | flops 15300820992 | bytes 3342336 | tf_op jit(solution)/shard_map/attention/pallas_call | solution.py:258
  80.6 16.6 %collective-permute-done.1.refs_0_ = bf16[2,64,2048]{2,1,0:T(8,128)(2,1)S(1)} collective-permute-done((bf16[2,64,2048]{2,1,0:T(8,128)(2,1)}, bf16[2,64,2048]{2,1,0:T(8,128)(2,1)S(1)}, u32[]{:S(2)}, u32[]{:S(2)}) %collective-permute-start.1) | collective-permute-done | bytes 524320 | tf_op jit(solution)/shard_map/ppermute | solution.py:592
  97.2 35.4 %collective-permute-start.25 = (bf16[256,2048]{1,0:T(8,128)(2,1)S(1)}, bf16[256,2048]{1,0:T(8,128)(2,1)S(1)}, u32[]{:S(2)}, u32[]{:S(2)}) collective-permute-start(bf16[256,2048]{1,0:T(8,128)(2,1)S(1)} %copy-done.7), channel_id=1, source_target_pairs={{0,8},{4,12},{24,16},{28,20},{1,9},{5,13},{25,17},{29,21},{2,10},{... | collective-permute-start | bytes 3145736 | tf_op jit(solution)/shard_map/ppermute | solution.py:594
  132.6 0.6 collective-permute-start.28
  133.2 1.5 collective-permute-start.29
  134.7 0.5 collective-permute-start.31
  135.2 11.5 %attention.4 = (f32[256,256]{1,0:T(8,128)S(1)}, f32[256,128]{1,0:T(8,128)S(1)}, bf16[48,4096]{1,0:T(8,128)(2,1)S(1)}, bf16[48,4096]{1,0:T(8,128)(2,1)}, bf16[48,...) custom-call(bf16[2,64,2048]{2,1,0:T(8,128)(2,1)S(1)} %collective-permute-done.11.refs_0_, ...), custom_call_target="tpu_custom_call" | custom-call | flops 20535312384 | bytes 2293760 | tf_op jit(solution)/shard_map/attention/pallas_call | solution.py:258
  146.7 32.5 %collective-permute-done.28.refs_19_ = bf16[256,2048]{1,0:T(8,128)(2,1)S(1)} collective-permute-done((bf16[256,2048]{1,0:T(8,128)(2,1)S(1)}, bf16[256,2048]{1,0:T(8,128)(2,1)S(1)}, u32[]{:S(2)}, u32[]{:S(2)}) %collective-permute-start.28) | collective-permute-done | bytes 1048608 | tf_op jit(solution)/shard_map/ppermute | solution.py:633
  179.3 0.5 collective-permute-start.33
  179.8 0.5 collective-permute-start.19
  180.3 0.5 collective-permute-start.20
  180.8 2.4 %collective-permute-start.21 = (bf16[48,4096]{1,0:T(8,128)(2,1)S(1)}, bf16[48,4096]{1,0:T(8,128)(2,1)S(1)}, u32[]{:S(2)}, u32[]{:S(2)}) collective-permute-start(bf16[48,4096]{1,0:T(8,128)(2,1)S(1)} %get-tuple-element.85), channel_id=1, source_target_pairs={{0,3},{1,2},{2,1},{3,0},{4,7},{5,6},{6,5},{7,4},{8,11},{9,10},{10,... | collective-permute-start | bytes 1179656 | tf_op jit(solution)/shard_map/ppermute | solution.py:657
  183.3 1.0 copy-done.6
  184.3 9.5 %attention.5 = (f32[256,256]{1,0:T(8,128)S(1)}, f32[256,128]{1,0:T(8,128)S(1)}, bf16[16,4096]{1,0:T(8,128)(2,1)S(1)}, bf16[16,4096]{1,0:T(8,128)(2,1)S(1)}, bf16...) custom-call(bf16[2,64,2048]{2,1,0:T(8,128)(2,1)S(1)} %copy-done.6, bf16[4,64,2048]{2,1,0:T(8,128)(2,1)S(1)} %bitcast.15, ...), custom_call_target="tpu_custom_call" | custom-call | flops 11945377792 | bytes 2293760 | tf_op jit(solution)/shard_map/attention/pallas_call | solution.py:258
  193.9 0.1 collective-permute-start.15
  194.0 0.6 collective-permute-start.22
  194.6 0.7 collective-permute-done.15.recv_ref
  195.3 0.5 collective-permute-start.23
  195.8 6.5 %collective-permute-done.22.refs_12_ = bf16[16,4096]{1,0:T(8,128)(2,1)S(1)} collective-permute-done((bf16[16,4096]{1,0:T(8,128)(2,1)S(1)}, bf16[16,4096]{1,0:T(8,128)(2,1)S(1)}, u32[]{:S(2)}, u32[]{:S(2)}) %collective-permute-start.22) | collective-permute-done | bytes 131104 | tf_op jit(solution)/shard_map/ppermute | solution.py:657
  202.3 0.5 collective-permute-start.24
  202.8 0.2 share.1
  203.1 1.6 collective-permute-start.16
  204.6 3.6 %collective-permute-done.24.refs_14_ = bf16[16,4096]{1,0:T(8,128)(2,1)S(1)} collective-permute-done((bf16[16,4096]{1,0:T(8,128)(2,1)S(1)}, bf16[16,4096]{1,0:T(8,128)(2,1)S(1)}, u32[]{:S(2)}, u32[]{:S(2)}) %collective-permute-start.24) | collective-permute-done | bytes 131104 | tf_op jit(solution)/shard_map/ppermute | solution.py:657
  208.2 0.5 collective-permute-start.17
  208.7 1.5 collective-permute-start.18
  210.3 1.8 collective-permute-done.17.refs_5_
  212.1 1.5 collective-permute-done.18.refs_6_
  213.6 6.1 %finish.1 = bf16[64,4096]{1,0:T(8,128)(2,1)} custom-call(bf16[1,4096]{1,0:T(2,128)(2,1)S(1)} %broadcast_select_fusion.refs_0_, bf16[64,4096]{1,0:T(8,128)(2,1)S(1)} %copy-done, bf16[64,4096]{1,0:T(8,128)(2,1)S(1)} %copy-done.1, bf16[64,256]{1,0:T(8,128)(2,1)S(1)} %get-tuple-element.78.refs_3_, bf16[64,256]{1,0:T(8,128)(2,1)S(1)} %collective-permute-done.16.refs_4_, ...), custom_call_target="tpu_custom_call" | custom-call | flops 1073741824 | bytes 8388608 | tf_op jit(solution)/shard_map/finish/pallas_call | solution.py:508
  (55 shorter events, 0.2 us)
Async XLA Ops:
  6.6 1.0 copy-start.2
  7.6 1.0 copy-start.3
  9.4 12.6 %copy-start.9 = (s32[256]{0:T(256)S(1)}, s32[256]{0:T(256)}, u32[]{:S(2)}) copy-start(s32[256]{0:T(256)} %param.18) | copy-start | bytes 3076
  9.4 12.6 %copy-start.10 = (s32[256]{0:T(256)S(1)}, s32[256]{0:T(256)}, u32[]{:S(2)}) copy-start(s32[256]{0:T(256)} %param.19) | copy-start | bytes 3076
  9.4 14.0 %copy-start.8 = (bf16[2048]{0:T(1024)(128)(2,1)S(1)}, bf16[2048]{0:T(1024)(128)(2,1)}, u32[]{:S(2)}) copy-start(bf16[2048]{0:T(1024)(128)(2,1)} %param.23) | copy-start | bytes 12292
  9.4 58.9 %copy-start.4 = (bf16[256,2048]{1,0:T(8,128)(2,1)S(1)}, bf16[256,2048]{1,0:T(8,128)(2,1)}, u32[]{:S(2)}) copy-start(bf16[256,2048]{1,0:T(8,128)(2,1)} %param.13) | copy-start | bytes 3145732
  17.5 117.2 %collective-permute-start.14 = (bf16[2048,2048]{1,0:T(8,128)(2,1)}, bf16[2048,2048]{1,0:T(8,128)(2,1)}, u32[]{:S(2)}, u32[]{:S(2)}) collective-permute-start(bf16[2048,2048]{1,0:T(8,128)(2,1)} %transposed.1.refs_8_.refs_7_), channel_id=1, source_target_pairs={{0,4},{4,0},{8,12},{12,8},{16,20},{20,16},{24,28},{28,24},{1,5},{5... | collective-permute-start | bytes 25165832 | tf_op jit(solution)/shard_map/ppermute | solution.py:566
  18.0 21.9 %collective-permute-start.2 = (bf16[2,320,128]{2,1,0:T(8,128)(2,1)}, bf16[2,320,128]{2,1,0:T(8,128)(2,1)S(1)}, u32[]{:S(2)}, u32[]{:S(2)}) collective-permute-start(bf16[2,320,128]{2,1,0:T(8,128)(2,1)} %get-tuple-element.64), channel_id=1, source_target_pairs={{0,1},{1,0},{2,3},{3,2},{4,5},{5,4},{6,7},{7,6},{8,9},{9,8},{10,11... | collective-permute-start | bytes 491528 | tf_op jit(solution)/shard_map/ppermute | solution.py:605
  20.5 19.4 %collective-permute-start.3 = (bf16[2,320,128]{2,1,0:T(8,128)(2,1)}, bf16[2,320,128]{2,1,0:T(8,128)(2,1)S(1)}, u32[]{:S(2)}, u32[]{:S(2)}) collective-permute-start(bf16[2,320,128]{2,1,0:T(8,128)(2,1)} %get-tuple-element.65), channel_id=1, source_target_pairs={{0,2},{1,3},{2,0},{3,1},{4,6},{5,7},{6,4},{7,5},{8,10},{9,11},{10,... | collective-permute-start | bytes 491528 | tf_op jit(solution)/shard_map/ppermute | solution.py:605
  22.0 9.1 %collective-permute-start.9 = (s32[256]{0:T(256)S(1)}, s32[256]{0:T(256)S(1)}, u32[]{:S(2)}, u32[]{:S(2)}) collective-permute-start(s32[256]{0:T(256)S(1)} %copy-done.9), channel_id=1, source_target_pairs={{0,4},{4,0},{8,12},{12,8},{16,20},{20,16},{24,28},{28,24},{1,5},{5... | collective-permute-start | bytes 3080 | tf_op jit(solution)/shard_map/ppermute | solution.py:566
  22.0 13.0 %collective-permute-start.10 = (s32[256]{0:T(256)S(1)}, s32[256]{0:T(256)S(1)}, u32[]{:S(2)}, u32[]{:S(2)}) collective-permute-start(s32[256]{0:T(256)S(1)} %copy-done.10), channel_id=1, source_target_pairs={{0,4},{4,0},{8,12},{12,8},{16,20},{20,16},{24,28},{28,24},{1,5},{5... | collective-permute-start | bytes 3080 | tf_op jit(solution)/shard_map/ppermute | solution.py:566
  31.1 9.0 %collective-permute-start.4 = (bf16[2,320,128]{2,1,0:T(8,128)(2,1)S(1)}, bf16[2,320,128]{2,1,0:T(8,128)(2,1)S(1)}, u32[]{:S(2)}, u32[]{:S(2)}) collective-permute-start(bf16[2,320,128]{2,1,0:T(8,128)(2,1)S(1)} %get-tuple-element.66), channel_id=1, source_target_pairs={{0,3},{1,2},{2,1},{3,0},{4,7},{5,6},{6,5},{7,4},{8,11},{9,10},{10,... | collective-permute-start | bytes 491528 | tf_op jit(solution)/shard_map/ppermute | solution.py:605
  35.0 1.2 collective-permute-start
  36.2 31.5 %collective-permute-start.13 = (bf16[128,2048]{1,0:T(8,128)(2,1)S(1)}, bf16[128,2048]{1,0:T(8,128)(2,1)S(1)}, u32[]{:S(2)}, u32[]{:S(2)}) collective-permute-start(bf16[128,2048]{1,0:T(8,128)(2,1)S(1)} %bitcast.18), channel_id=1, source_target_pairs={{0,24},{4,28},{8,16},{12,20},{16,8},{20,12},{24,0},{28,4},{1,25},{... | collective-permute-start | bytes 1572872 | tf_op jit(solution)/shard_map/ppermute | solution.py:592
  39.9 1.4 collective-permute-start.5
  39.9 24.3 %collective-permute-start.12 = (bf16[128,2048]{1,0:T(8,128)(2,1)}, bf16[128,2048]{1,0:T(8,128)(2,1)S(1)}, u32[]{:S(2)}, u32[]{:S(2)}) collective-permute-start(bf16[128,2048]{1,0:T(8,128)(2,1)} %bitcast.19), channel_id=1, source_target_pairs={{0,24},{4,28},{8,16},{12,20},{16,8},{20,12},{24,0},{28,4},{1,25},{... | collective-permute-start | bytes 1572872 | tf_op jit(solution)/shard_map/ppermute | solution.py:592
  40.2 1.4 collective-permute-start.6
  41.2 1.4 collective-permute-start.7
  41.5 4.1 %collective-permute-start.8 = (bf16[2,320,128]{2,1,0:T(8,128)(2,1)S(1)}, bf16[2,320,128]{2,1,0:T(8,128)(2,1)S(1)}, u32[]{:S(2)}, u32[]{:S(2)}) collective-permute-start(bf16[2,320,128]{2,1,0:T(8,128)(2,1)S(1)} %collective-permute-done.4.refs_3_), channel_id=1, source_target_pairs={{0,4},{4,0},{8,12},{12,8},{16,20},{20,16},{24,28},{28,24},{1,5},{5... | collective-permute-start | bytes 491528 | tf_op jit(solution)/shard_map/ppermute | solution.py:566
  42.6 90.0 %collective-permute-start.11 = (bf16[2,64,2048]{2,1,0:T(8,128)(2,1)}, bf16[2,64,2048]{2,1,0:T(8,128)(2,1)S(1)}, u32[]{:S(2)}, u32[]{:S(2)}) collective-permute-start(bf16[2,64,2048]{2,1,0:T(8,128)(2,1)} %get-tuple-element.68), channel_id=1, source_target_pairs={{0,24},{4,28},{8,16},{12,20},{16,8},{20,12},{24,0},{28,4},{1,25},{... | collective-permute-start | bytes 1572872 | tf_op jit(solution)/shard_map/ppermute | solution.py:592
  45.6 87.6 %collective-permute-start.26 = (bf16[2,64,2048]{2,1,0:T(8,128)(2,1)}, bf16[2,64,2048]{2,1,0:T(8,128)(2,1)S(1)}, u32[]{:S(2)}, u32[]{:S(2)}) collective-permute-start(bf16[2,64,2048]{2,1,0:T(8,128)(2,1)} %get-tuple-element.68), channel_id=1, source_target_pairs={{0,8},{4,12},{24,16},{28,20},{1,9},{5,13},{25,17},{29,21},{2,10},{... | collective-permute-start | bytes 1572872 | tf_op jit(solution)/shard_map/ppermute | solution.py:594
  64.2 33.0 %collective-permute-start.1 = (bf16[2,64,2048]{2,1,0:T(8,128)(2,1)}, bf16[2,64,2048]{2,1,0:T(8,128)(2,1)S(1)}, u32[]{:S(2)}, u32[]{:S(2)}) collective-permute-start(bf16[2,64,2048]{2,1,0:T(8,128)(2,1)} %get-tuple-element.54), channel_id=1, source_target_pairs={{0,24},{4,28},{8,16},{12,20},{16,8},{20,12},{24,0},{28,4},{1,25},{... | collective-permute-start | bytes 1572872 | tf_op jit(solution)/shard_map/ppermute | solution.py:592
  67.8 66.9 %collective-permute-start.27 = (bf16[256,2048]{1,0:T(8,128)(2,1)S(1)}, bf16[256,2048]{1,0:T(8,128)(2,1)S(1)}, u32[]{:S(2)}, u32[]{:S(2)}) collective-permute-start(bf16[256,2048]{1,0:T(8,128)(2,1)S(1)} %bitcast.8), channel_id=1, source_target_pairs={{0,1},{1,0},{2,3},{3,2},{4,5},{5,4},{6,7},{7,6},{8,9},{9,8},{10,11... | collective-permute-start | bytes 3145736 | tf_op jit(solution)/shard_map/ppermute | solution.py:633
  68.3 28.9 %copy-start.7 = (bf16[256,2048]{1,0:T(8,128)(2,1)S(1)}, bf16[256,2048]{1,0:T(8,128)(2,1)}, u32[]{:S(2)}) copy-start(bf16[256,2048]{1,0:T(8,128)(2,1)} %q_ref) | copy-start | bytes 3145732
  97.2 49.5 %copy-start.5 = (bf16[2,64,2048]{2,1,0:T(8,128)(2,1)}, bf16[2,64,2048]{2,1,0:T(8,128)(2,1)S(1)}, u32[]{:S(2)}) copy-start(bf16[2,64,2048]{2,1,0:T(8,128)(2,1)S(1)} %collective-permute-done.1.refs_0_) | copy-start | bytes 1572868
  97.2 82.6 %collective-permute-start.25 = (bf16[256,2048]{1,0:T(8,128)(2,1)S(1)}, bf16[256,2048]{1,0:T(8,128)(2,1)S(1)}, u32[]{:S(2)}, u32[]{:S(2)}) collective-permute-start(bf16[256,2048]{1,0:T(8,128)(2,1)S(1)} %copy-done.7), channel_id=1, source_target_pairs={{0,8},{4,12},{24,16},{28,20},{1,9},{5,13},{25,17},{29,21},{2,10},{... | collective-permute-start | bytes 3145736 | tf_op jit(solution)/shard_map/ppermute | solution.py:594
  132.6 46.6 %collective-permute-start.28 = (bf16[256,2048]{1,0:T(8,128)(2,1)S(1)}, bf16[256,2048]{1,0:T(8,128)(2,1)S(1)}, u32[]{:S(2)}, u32[]{:S(2)}) collective-permute-start(bf16[256,2048]{1,0:T(8,128)(2,1)S(1)} %bitcast.9), channel_id=1, source_target_pairs={{0,2},{1,3},{2,0},{3,1},{4,6},{5,7},{6,4},{7,5},{8,10},{9,11},{10,... | collective-permute-start | bytes 3145736 | tf_op jit(solution)/shard_map/ppermute | solution.py:633
  133.2 46.1 %collective-permute-start.29 = (bf16[256,2048]{1,0:T(8,128)(2,1)S(1)}, bf16[256,2048]{1,0:T(8,128)(2,1)S(1)}, u32[]{:S(2)}, u32[]{:S(2)}) collective-permute-start(bf16[256,2048]{1,0:T(8,128)(2,1)S(1)} %bitcast.10), channel_id=1, source_target_pairs={{0,3},{1,2},{2,1},{3,0},{4,7},{5,6},{6,5},{7,4},{8,11},{9,10},{10,... | collective-permute-start | bytes 3145736 | tf_op jit(solution)/shard_map/ppermute | solution.py:633
  134.7 45.6 %collective-permute-start.30 = (bf16[256,2048]{1,0:T(8,128)(2,1)S(1)}, bf16[256,2048]{1,0:T(8,128)(2,1)S(1)}, u32[]{:S(2)}, u32[]{:S(2)}) collective-permute-start(bf16[256,2048]{1,0:T(8,128)(2,1)S(1)} %bitcast.11), channel_id=1, source_target_pairs={{0,4},{4,0},{8,12},{12,8},{16,20},{20,16},{24,28},{28,24},{1,5},{5... | collective-permute-start | bytes 3145736 | tf_op jit(solution)/shard_map/ppermute | solution.py:566
  134.7 46.1 %collective-permute-start.31 = (bf16[256,2048]{1,0:T(8,128)(2,1)S(1)}, bf16[256,2048]{1,0:T(8,128)(2,1)S(1)}, u32[]{:S(2)}, u32[]{:S(2)}) collective-permute-start(bf16[256,2048]{1,0:T(8,128)(2,1)S(1)} %collective-permute-done.27.refs_18_), channel_id=1, source_target_pairs={{0,4},{4,0},{8,12},{12,8},{16,20},{20,16},{24,28},{28,24},{1,5},{5... | collective-permute-start | bytes 3145736 | tf_op jit(solution)/shard_map/ppermute | solution.py:566
  179.3 14.6 %collective-permute-start.32 = (bf16[256,2048]{1,0:T(8,128)(2,1)S(1)}, bf16[256,2048]{1,0:T(8,128)(2,1)S(1)}, u32[]{:S(2)}, u32[]{:S(2)}) collective-permute-start(bf16[256,2048]{1,0:T(8,128)(2,1)S(1)} %collective-permute-done.28.refs_19_), channel_id=1, source_target_pairs={{0,4},{4,0},{8,12},{12,8},{16,20},{20,16},{24,28},{28,24},{1,5},{5... | collective-permute-start | bytes 3145736 | tf_op jit(solution)/shard_map/ppermute | solution.py:566
  179.3 14.7 %collective-permute-start.33 = (bf16[256,2048]{1,0:T(8,128)(2,1)S(1)}, bf16[256,2048]{1,0:T(8,128)(2,1)S(1)}, u32[]{:S(2)}, u32[]{:S(2)}) collective-permute-start(bf16[256,2048]{1,0:T(8,128)(2,1)S(1)} %collective-permute-done.29.refs_20_), channel_id=1, source_target_pairs={{0,4},{4,0},{8,12},{12,8},{16,20},{20,16},{24,28},{28,24},{1,5},{5... | collective-permute-start | bytes 3145736 | tf_op jit(solution)/shard_map/ppermute | solution.py:566
  179.8 33.8 %collective-permute-start.19 = (bf16[48,4096]{1,0:T(8,128)(2,1)}, bf16[48,4096]{1,0:T(8,128)(2,1)S(1)}, u32[]{:S(2)}, u32[]{:S(2)}) collective-permute-start(bf16[48,4096]{1,0:T(8,128)(2,1)} %get-tuple-element.83), channel_id=1, source_target_pairs={{0,1},{1,0},{2,3},{3,2},{4,5},{5,4},{6,7},{7,6},{8,9},{9,8},{10,11... | collective-permute-start | bytes 1179656 | tf_op jit(solution)/shard_map/ppermute | solution.py:657
  180.3 33.2 %collective-permute-start.20 = (bf16[48,4096]{1,0:T(8,128)(2,1)}, bf16[48,4096]{1,0:T(8,128)(2,1)S(1)}, u32[]{:S(2)}, u32[]{:S(2)}) collective-permute-start(bf16[48,4096]{1,0:T(8,128)(2,1)} %get-tuple-element.84), channel_id=1, source_target_pairs={{0,2},{1,3},{2,0},{3,1},{4,6},{5,7},{6,4},{7,5},{8,10},{9,11},{10,... | collective-permute-start | bytes 1179656 | tf_op jit(solution)/shard_map/ppermute | solution.py:657
  180.8 32.7 %collective-permute-start.21 = (bf16[48,4096]{1,0:T(8,128)(2,1)S(1)}, bf16[48,4096]{1,0:T(8,128)(2,1)S(1)}, u32[]{:S(2)}, u32[]{:S(2)}) collective-permute-start(bf16[48,4096]{1,0:T(8,128)(2,1)S(1)} %get-tuple-element.85), channel_id=1, source_target_pairs={{0,3},{1,2},{2,1},{3,0},{4,7},{5,6},{6,5},{7,4},{8,11},{9,10},{10,... | collective-permute-start | bytes 1179656 | tf_op jit(solution)/shard_map/ppermute | solution.py:657
  183.3 1.0 copy-start.6
  184.3 29.3 %copy-start = (bf16[64,4096]{1,0:T(8,128)(2,1)S(1)}, bf16[64,4096]{1,0:T(8,128)(2,1)}, u32[]{:S(2)}) copy-start(bf16[64,4096]{1,0:T(8,128)(2,1)} %refs_1_.2) | copy-start | bytes 1572868
  184.3 29.3 %copy-start.1 = (bf16[64,4096]{1,0:T(8,128)(2,1)S(1)}, bf16[64,4096]{1,0:T(8,128)(2,1)}, u32[]{:S(2)}) copy-start(bf16[64,4096]{1,0:T(8,128)(2,1)} %refs_2_.1) | copy-start | bytes 1572868
  193.9 1.4 collective-permute-start.15
  194.0 8.4 %collective-permute-start.22 = (bf16[16,4096]{1,0:T(8,128)(2,1)S(1)}, bf16[16,4096]{1,0:T(8,128)(2,1)S(1)}, u32[]{:S(2)}, u32[]{:S(2)}) collective-permute-start(bf16[16,4096]{1,0:T(8,128)(2,1)S(1)} %get-tuple-element.87), channel_id=1, source_target_pairs={{0,1},{1,0},{2,3},{3,2},{4,5},{5,4},{6,7},{7,6},{8,9},{9,8},{10,11... | collective-permute-start | bytes 393224 | tf_op jit(solution)/shard_map/ppermute | solution.py:657
  195.3 7.8 %collective-permute-start.23 = (bf16[16,4096]{1,0:T(8,128)(2,1)S(1)}, bf16[16,4096]{1,0:T(8,128)(2,1)S(1)}, u32[]{:S(2)}, u32[]{:S(2)}) collective-permute-start(bf16[16,4096]{1,0:T(8,128)(2,1)S(1)} %get-tuple-element.88), channel_id=1, source_target_pairs={{0,2},{1,3},{2,0},{3,1},{4,6},{5,7},{6,4},{7,5},{8,10},{9,11},{10,... | collective-permute-start | bytes 393224 | tf_op jit(solution)/shard_map/ppermute | solution.py:657
  202.3 5.9 %collective-permute-start.24 = (bf16[16,4096]{1,0:T(8,128)(2,1)S(1)}, bf16[16,4096]{1,0:T(8,128)(2,1)S(1)}, u32[]{:S(2)}, u32[]{:S(2)}) collective-permute-start(bf16[16,4096]{1,0:T(8,128)(2,1)S(1)} %get-tuple-element.89), channel_id=1, source_target_pairs={{0,3},{1,2},{2,1},{3,0},{4,7},{5,6},{6,5},{7,4},{8,11},{9,10},{10,... | collective-permute-start | bytes 393224 | tf_op jit(solution)/shard_map/ppermute | solution.py:657
  203.1 5.7 %collective-permute-start.16 = (bf16[64,256]{1,0:T(8,128)(2,1)S(1)}, bf16[64,256]{1,0:T(8,128)(2,1)S(1)}, u32[]{:S(2)}, u32[]{:S(2)}) collective-permute-start(bf16[64,256]{1,0:T(8,128)(2,1)S(1)} %get-tuple-element.79), channel_id=1, source_target_pairs={{0,1},{1,0},{2,3},{3,2},{4,5},{5,4},{6,7},{7,6},{8,9},{9,8},{10,11... | collective-permute-start | bytes 98312 | tf_op jit(solution)/shard_map/ppermute | solution.py:664
  208.2 3.9 %collective-permute-start.17 = (bf16[64,256]{1,0:T(8,128)(2,1)S(1)}, bf16[64,256]{1,0:T(8,128)(2,1)S(1)}, u32[]{:S(2)}, u32[]{:S(2)}) collective-permute-start(bf16[64,256]{1,0:T(8,128)(2,1)S(1)} %get-tuple-element.80), channel_id=1, source_target_pairs={{0,2},{1,3},{2,0},{3,1},{4,6},{5,7},{6,4},{7,5},{8,10},{9,11},{10,... | collective-permute-start | bytes 98312 | tf_op jit(solution)/shard_map/ppermute | solution.py:664
  208.7 4.8 %collective-permute-start.18 = (bf16[64,256]{1,0:T(8,128)(2,1)S(1)}, bf16[64,256]{1,0:T(8,128)(2,1)S(1)}, u32[]{:S(2)}, u32[]{:S(2)}) collective-permute-start(bf16[64,256]{1,0:T(8,128)(2,1)S(1)} %get-tuple-element.81), channel_id=1, source_target_pairs={{0,3},{1,2},{2,1},{3,0},{4,7},{5,6},{6,5},{7,4},{8,11},{9,10},{10,... | collective-permute-start | bytes 98312 | tf_op jit(solution)/shard_map/ppermute | solution.py:664
